TPU v7x, 32 devices: a 4x4x1 block of a 4x4x8 slice. The times are simulated.
32 devices in a mesh: prob: 1 (over z), samp: 4 (over y), feat: 8 (over x, core).
Axes of the slice: x: 4, y: 4, z: 1, core: 2. Of those that a mesh axis runs over, the one named last changes fastest.
The devices are a block of a 4x4x8 slice.
Arguments:
- x_mat: bfloat16 [512, 1048576], P(('prob', 'samp'), 'feat')
- w_init: float32 [1048576, 32], P(('prob', 'feat'))
- targets: float32 [512, 32], P(('prob', 'samp'))
- step_size: float32 [1048576], P(('prob', 'feat'))
Outputs:
- output 1: float32 [1048576, 32], P(('prob', 'feat'))
- output 2: float32 [512, 32], P(('prob', 'samp'))
All inputs are finite; a program needn't handle non-finite values.
Results may differ from a plain program's by a relative error of at most 0.00281675.
Values are sent between devices in bfloat16 or wider.
A program may use at most 768 MiB of HBM per device.

v0:
```python
import jax
import jax.numpy as jnp
from jax import lax
from jax.sharding import PartitionSpec as P, NamedSharding

SWEEPS = 4
COMBINE_WEIGHT = 0.8
RIDGE_SCALE = 0.1


def solution(mesh):
    samp_count = mesh.shape["samp"]
    feat_count = mesh.shape["feat"]

    def local_solve(x_loc, w_loc, y_loc, eta_loc):
        rows_loc, feat_len = x_loc.shape
        samples = rows_loc * samp_count
        ridge = RIDGE_SCALE * (feat_len * feat_count) / samples
        first = jnp.dot(x_loc, w_loc.astype(jnp.bfloat16), preferred_element_type=jnp.float32)
        residual = y_loc - lax.psum(first.astype(jnp.bfloat16).astype(jnp.float32), "feat")
        weights = w_loc
        for sweep in range(SWEEPS):
            part_grad = lax.dot_general(x_loc, residual.astype(jnp.bfloat16), (((0,), (0,)), ((), ())), preferred_element_type=jnp.float32)
            gradient = lax.psum(part_grad, "samp") / samples
            delta = eta_loc[:, None] * (gradient - ridge * weights)
            weights = weights + COMBINE_WEIGHT * delta
            update = jnp.dot(x_loc, delta.astype(jnp.bfloat16), preferred_element_type=jnp.float32)
            residual = residual - COMBINE_WEIGHT * lax.psum(update.astype(jnp.bfloat16).astype(jnp.float32), "feat")
        return weights, residual

    return jax.shard_map(
        local_solve,
        mesh=mesh,
        in_specs=(P(("prob", "samp"), "feat"), P(("prob", "feat"), None), P(("prob", "samp"), None), P(("prob", "feat"))),
        out_specs=(P(("prob", "feat"), None), P(("prob", "samp"), None)),
        check_vma=False,
    )
```

profile of v0, /device:TPU:97, one launch (start us, length us, event | category | flops | bytes accessed | tf_op | source)
XLA Modules:
  0.0 1518.7 jit_solution(10885880576125348235)
XLA Ops:
  7.2 0.0 copy-start.1
  7.2 0.1 all-reduce.5.cloned.1.call-start
  7.3 21.0 %fusion.29 = f32[128,32]{0,1:T(8,128)S(1)} fusion(bf16[128,131072]{1,0:T(8,128)(2,1)} %param.4, f32[131072,32]{0,1:T(8,128)} %param.5), kind=kOutput, calls=%fused_computation.35 | convolution fusion | flops 1077944320 | bytes 50348032 | tf_op jit(solution)/shard_map/dot_general | solution.py:19
  28.3 24.0 %psum.63 = f32[128,32]{0,1:T(8,128)S(1)} all-reduce(f32[128,32]{0,1:T(8,128)S(1)} %fusion.29), channel_id=1, replica_groups=mesh['prob'=1,'samp'=4,'feat'=8] {'feat'}, use_global_device_ids=true, to_apply=%region_0.0 | all-reduce | flops 4096 | bytes 32768 | tf_op jit(solution)/shard_map/psum | solution.py:20
  52.3 0.0 copy-done.1
  52.3 19.3 %convolution_bitcast_fusion.3 = f32[131072,32]{0,1:T(8,128)} fusion(bf16[128,131072]{1,0:T(8,128)(2,1)} %param.4, f32[128,32]{0,1:T(8,128)S(1)} %sub.27), kind=kOutput, calls=%fused_computation.3 | convolution fusion | flops 1073745920 | bytes 50348032 | tf_op jit(solution)/shard_map/dot_general | solution.py:23
  71.6 0.0 copy-start
  71.6 0.1 all-reduce.5.cloned.1.call-update
  71.7 0.1 all-reduce.7.cloned.1.call-start
  71.8 293.3 %all-reduce.5.cloned.1.call-done = f32[131072,32]{0,1:T(8,128)} async-done(((f32[131072,32]{0,1:T(8,128)}), f32[131072,32]{0,1:T(8,128)}) %all-reduce.5.cloned.1.call-update) | async-done | bytes 16777232 | tf_op jit(solution)/shard_map/psum | solution.py:24
  365.1 0.0 copy-done
  365.1 23.3 %fusion.38 = f32[128,32]{0,1:T(8,128)S(1)} fusion(bf16[128,131072]{1,0:T(8,128)(2,1)} %param.4, f32[131072,32]{0,1:T(8,128)} %param.5, f32[131072,32]{0,1:T(8,128)} %all-reduce.5.cloned.1.call-done, f32[131072]{0:T(1024)S(1)} %copy-done), kind=kOutput, calls=%fused_computation.38 | convolution fusion | flops 1094721536 | bytes 67649536 | tf_op jit(solution)/shard_map/dot_general | solution.py:27
  388.4 22.7 %psum.65 = f32[128,32]{0,1:T(8,128)S(1)} all-reduce(f32[128,32]{0,1:T(8,128)S(1)} %fusion.38), channel_id=1, replica_groups=mesh['prob'=1,'samp'=4,'feat'=8] {'feat'}, use_global_device_ids=true, to_apply=%region_2.0 | all-reduce | flops 4096 | bytes 32768 | tf_op jit(solution)/shard_map/psum | solution.py:28
  411.1 19.3 %convolution_bitcast_fusion.2 = f32[131072,32]{0,1:T(8,128)} fusion(bf16[128,131072]{1,0:T(8,128)(2,1)} %param.4, f32[128,32]{0,1:T(8,128)S(1)} %sub.27, f32[128,32]{0,1:T(8,128)S(1)} %psum.65), kind=kOutput, calls=%fused_computation.2 | convolution fusion | flops 1073754112 | bytes 50364416 | tf_op jit(solution)/shard_map/dot_general | solution.py:23
  430.4 0.1 all-reduce.7.cloned.1.call-update
  430.5 0.1 all-reduce.9.cloned.1.call-start
  430.5 290.3 %all-reduce.7.cloned.1.call-done = f32[131072,32]{0,1:T(8,128)} async-done(((f32[131072,32]{0,1:T(8,128)}), f32[131072,32]{0,1:T(8,128)}) %all-reduce.7.cloned.1.call-update) | async-done | bytes 16777232 | tf_op jit(solution)/shard_map/psum | solution.py:24
  720.9 28.2 %fusion.56 = f32[128,32]{0,1:T(8,128)S(1)} fusion(bf16[128,131072]{1,0:T(8,128)(2,1)} %param.4, f32[131072,32]{0,1:T(8,128)} %all-reduce.7.cloned.1.call-done, f32[131072]{0:T(1024)S(1)} %copy-done, f32[131072,32]{0,1:T(8,128)} %param.5, f32[131072,32]{0,1:T(8,128)} %all-reduce.5.cloned.1.call-done), kind=kOutput, calls=%fused_computation.44 | convolution fusion | flops 1119887360 | bytes 84426752 | tf_op jit(solution)/shard_map/dot_general | solution.py:27
  749.0 22.7 %psum.67 = f32[128,32]{0,1:T(8,128)S(1)} all-reduce(f32[128,32]{0,1:T(8,128)S(1)} %fusion.56), channel_id=1, replica_groups=mesh['prob'=1,'samp'=4,'feat'=8] {'feat'}, use_global_device_ids=true, to_apply=%region_4.0 | all-reduce | flops 4096 | bytes 32768 | tf_op jit(solution)/shard_map/psum | solution.py:28
  771.8 19.1 %convolution_bitcast_fusion.1 = f32[131072,32]{0,1:T(8,128)} fusion(bf16[128,131072]{1,0:T(8,128)(2,1)} %param.4, f32[128,32]{0,1:T(8,128)S(1)} %multiply_subtract_fusion.2), kind=kOutput, calls=%fused_computation.1 | convolution fusion | flops 1073745920 | bytes 50348032 | tf_op jit(solution)/shard_map/dot_general | solution.py:23
  790.8 0.1 all-reduce.9.cloned.1.call-update
  790.9 0.1 all-reduce.11.cloned.1.call-start
  791.0 23.8 %multiply_add_fusion.2 = f32[131072,32]{0,1:T(8,128)} fusion(f32[131072,32]{0,1:T(8,128)} %all-reduce.7.cloned.1.call-done, f32[131072]{0:T(1024)S(1)} %copy-done, f32[131072,32]{0,1:T(8,128)} %param.5, f32[131072,32]{0,1:T(8,128)} %all-reduce.5.cloned.1.call-done), kind=kLoop, calls=%fused_computation.8 | loop fusion | flops 50331648 | bytes 67633152 | tf_op jit(solution)/shard_map/add | solution.py:26
  814.8 266.5 %all-reduce.9.cloned.1.call-done = f32[131072,32]{0,1:T(8,128)} async-done(((f32[131072,32]{0,1:T(8,128)}), f32[131072,32]{0,1:T(8,128)}) %all-reduce.9.cloned.1.call-update) | async-done | bytes 16777232 | tf_op jit(solution)/shard_map/psum | solution.py:24
  1081.3 23.3 %fusion.47 = f32[128,32]{0,1:T(8,128)S(1)} fusion(bf16[128,131072]{1,0:T(8,128)(2,1)} %param.4, f32[131072,32]{0,1:T(8,128)} %multiply_add_fusion.2, f32[131072,32]{0,1:T(8,128)} %all-reduce.9.cloned.1.call-done, f32[131072]{0:T(1024)S(1)} %copy-done), kind=kOutput, calls=%fused_computation.41 | convolution fusion | flops 1094721536 | bytes 67649536 | tf_op jit(solution)/shard_map/dot_general | solution.py:27
  1104.6 22.7 %psum.69 = f32[128,32]{0,1:T(8,128)S(1)} all-reduce(f32[128,32]{0,1:T(8,128)S(1)} %fusion.47), channel_id=1, replica_groups=mesh['prob'=1,'samp'=4,'feat'=8] {'feat'}, use_global_device_ids=true, to_apply=%region_6.0 | all-reduce | flops 4096 | bytes 32768 | tf_op jit(solution)/shard_map/psum | solution.py:28
  1127.3 19.1 %convolution_bitcast_fusion = f32[131072,32]{0,1:T(8,128)} fusion(bf16[128,131072]{1,0:T(8,128)(2,1)} %param.4, f32[128,32]{0,1:T(8,128)S(1)} %multiply_subtract_fusion.2, f32[128,32]{0,1:T(8,128)S(1)} %psum.69), kind=kOutput, calls=%fused_computation | convolution fusion | flops 1073754112 | bytes 50364416 | tf_op jit(solution)/shard_map/dot_general | solution.py:23
  1146.4 0.1 all-reduce.11.cloned.1.call-update
  1146.4 290.4 %all-reduce.11.cloned.1.call-done = f32[131072,32]{0,1:T(8,128)} async-done(((f32[131072,32]{0,1:T(8,128)}), f32[131072,32]{0,1:T(8,128)}) %all-reduce.11.cloned.1.call-update) | async-done | bytes 16777232 | tf_op jit(solution)/shard_map/psum | solution.py:24
  1436.8 28.2 %fusion.65 = f32[128,32]{0,1:T(8,128)S(1)} fusion(bf16[128,131072]{1,0:T(8,128)(2,1)} %param.4, f32[131072,32]{0,1:T(8,128)} %all-reduce.11.cloned.1.call-done, f32[131072]{0:T(1024)S(1)} %copy-done, f32[131072,32]{0,1:T(8,128)} %multiply_add_fusion.2, f32[131072,32]{0,1:T(8,128)} %all-reduce.9.cloned.1.call-done), kind=kOutput, calls=%fused_computation.47 | convolution fusion | flops 1119887360 | bytes 84426752 | tf_op jit(solution)/shard_map/dot_general | solution.py:27
  1465.0 22.7 %psum.71 = f32[128,32]{0,1:T(8,128)S(1)} all-reduce(f32[128,32]{0,1:T(8,128)S(1)} %fusion.65), channel_id=1, replica_groups=mesh['prob'=1,'samp'=4,'feat'=8] {'feat'}, use_global_device_ids=true, to_apply=%region_8.0 | all-reduce | flops 4096 | bytes 32768 | tf_op jit(solution)/shard_map/psum | solution.py:28
  1487.7 0.6 multiply_subtract_fusion
  1488.3 23.8 %multiply_add_fusion = f32[131072,32]{0,1:T(8,128)} fusion(f32[131072,32]{0,1:T(8,128)} %all-reduce.11.cloned.1.call-done, f32[131072]{0:T(1024)S(1)} %copy-done, f32[131072,32]{0,1:T(8,128)} %multiply_add_fusion.2, f32[131072,32]{0,1:T(8,128)} %all-reduce.9.cloned.1.call-done), kind=kLoop, calls=%fused_computation.4 | loop fusion | flops 50331648 | bytes 67633152 | tf_op jit(solution)/shard_map/add | solution.py:26
  (2 shorter events, 0.0 us)
Async XLA Ops:
  7.2 45.2 %copy-start.1 = (f32[128,32]{0,1:T(8,128)S(1)}, f32[128,32]{0,1:T(8,128)}, u32[]{:S(2)}) copy-start(f32[128,32]{0,1:T(8,128)} %param.6) | copy-start | bytes 49156
  7.2 357.9 %all-reduce.5.cloned.1.call-start = ((), (), s32[]{:S(2)}) async-start(), calls=%async_computation | async-start | bytes 33554432 | tf_op jit(solution)/shard_map/psum | solution.py:24
  71.6 293.5 %copy-start = (f32[131072]{0:T(1024)S(1)}, f32[131072]{0:T(1024)}, u32[]{:S(2)}) copy-start(f32[131072]{0:T(1024)} %param.7) | copy-start | bytes 1572868
  71.7 649.2 %all-reduce.7.cloned.1.call-start = ((), (), s32[]{:S(2)}) async-start(), calls=%async_computation.1 | async-start | bytes 33554432 | tf_op jit(solution)/shard_map/psum | solution.py:24
  430.5 650.8 %all-reduce.9.cloned.1.call-start = ((), (), s32[]{:S(2)}) async-start(), calls=%async_computation.2 | async-start | bytes 33554432 | tf_op jit(solution)/shard_map/psum | solution.py:24
  790.9 645.9 %all-reduce.11.cloned.1.call-start = ((), (), s32[]{:S(2)}) async-start(), calls=%async_computation.3 | async-start | bytes 33554432 | tf_op jit(solution)/shard_map/psum | solution.py:24
Sparse Core Ops, SparseCore 0:
  71.8 293.2 all-reduce.4
  430.6 290.2 all-reduce.6
  791.0 290.2 all-reduce.8
  1146.6 290.2 all-reduce.10
where the time goes:
time: 1520 us
  waiting for transfers between devices  1140 us (75%)
  matrix products  201 us (13%)
  blocking collectives  115 us (8%)
  other arithmetic  48.2 us (3%)
    psum x4, waiting for transfers between devices, local_solve(): gradient = lax.psum(part_grad, 'samp') / samples  1140 us
    dot_general x4, matrix products, local_solve(): jnp.dot(x_loc, delta.astype(jnp.bfloat16), preferred_element_type=jnp.flo...  103 us
    psum x4, blocking collectives, local_solve(): lax.psum(update.astype(jnp.bfloat16).astype(jnp.float32), 'feat')  90.9 us
    dot_general x4, matrix products, local_solve(): lax.dot_general(x_loc, residual.astype(jnp.bfloat16), (((0,), (0,)), ((),...  76.8 us
    add x2, other arithmetic, local_solve(): weights = weights + COMBINE_WEIGHT * delta  47.6 us
  transfers between devices with their start and end apart: 4, of which 4 were waited for; matrix products, arithmetic and copies ran while one was open for 2% of the time, Pallas kernels for 0%

commit v1 on v0

v1 whole, which is shorter than its diff:
```python
import functools

import jax
import jax.numpy as jnp
from jax import lax
from jax.experimental import pallas as pl
from jax.experimental.pallas import tpu as pltpu
from jax.sharding import PartitionSpec as P

SWEEPS = 4
COMBINE_WEIGHT = 0.8
RIDGE_SCALE = 0.1
CHUNKS = 16
SUB = 512
V_SLOTS = 4
MESH = pl.DeviceIdType.MESH
NT = (((1,), (1,)), ((), ()))


def kernel(ns, nf, x_hbm, wt_hbm, yt_ref, eta_hbm, wout, rout, xbuf, relay, wbuf, ebuf, vx, vw, usend, rsbuf, agbuf, rbuf, rstate,
           own_sem, w_sem, e_sem, v_sem, rel_s, rel_r, dir_s, dir_r, fwd_s, fwd_r, a_s, a_r, b_s, b_r, c_s, c_r,
           wl_sem, wd_s, wd_r, wf_s, wf_r):
    y, f = lax.axis_index("samp"), lax.axis_index("feat")
    rows, feat_len = x_hbm.shape
    targets = wt_hbm.shape[0]
    own = feat_len // ns
    chunk = own // CHUNKS
    half = CHUNKS // 2
    sub = min(SUB, chunk)
    samples = rows * ns
    inv = 1.0 / samples
    ridge = RIDGE_SCALE * (feat_len * nf) / samples
    up, down, far = lax.rem(y + 1, ns), lax.rem(y + ns - 1, ns), lax.rem(y + 2, ns)
    ring = (up, down)

    def cols(owner, k):
        return pl.ds(pl.multiple_of(owner * own + k * chunk, chunk), chunk)

    def rows_of(s):
        return pl.ds(pl.multiple_of(s * rows, rows), rows)

    def remote(src, dst, send, recv, axis, dev):
        return pltpu.make_async_remote_copy(src_ref=src, dst_ref=dst, send_sem=send, recv_sem=recv,
                                            device_id={axis: dev}, device_id_type=MESH)

    def own_copy(k):
        return pltpu.make_async_copy(x_hbm.at[:, cols(y, k)], xbuf.at[k, rows_of(y), :], own_sem.at[k])

    def w_load(k):
        return pltpu.make_async_copy(wt_hbm.at[:, cols(y, k)], wbuf.at[k], w_sem.at[k])

    def e_load(k):
        return pltpu.make_async_copy(eta_hbm.at[:, cols(y, k)], ebuf.at[k], e_sem.at[k])

    v_steps = ns * CHUNKS

    def v_cols(k):
        return pl.ds(pl.multiple_of(k * chunk, chunk), chunk)

    def v_load(k, slot):
        return (pltpu.make_async_copy(x_hbm.at[:, v_cols(k)], vx.at[slot], v_sem.at[0, slot]),
                pltpu.make_async_copy(wt_hbm.at[:, v_cols(k)], vw.at[slot], v_sem.at[1, slot]))

    def relay_copy(d, i):
        return remote(x_hbm.at[:, cols(far, 2 * i + d)], relay.at[d, i], rel_s.at[d, i], rel_r.at[d, i], "samp", ring[d])

    def direct_copy(d, k, place):
        return remote(x_hbm.at[:, cols(ring[d], k)], xbuf.at[k, rows_of(place), :], dir_s.at[d, k], dir_r.at[d, k], "samp", ring[d])

    def forward_copy(d, i, place):
        return remote(relay.at[d, i], xbuf.at[2 * i + d, rows_of(place), :], fwd_s.at[d, i], fwd_r.at[d, i], "samp", ring[d])

    def wd_copy(d, k, owner):
        return remote(wbuf.at[k], wout.at[:, cols(owner, k)], wd_s.at[d, k], wd_r.at[d, k], "samp", ring[d])

    def wf_copy(d, i, owner):
        part = wout.at[:, cols(owner, 2 * i + d)]
        return remote(part, part, wf_s.at[d, i], wf_r.at[d, i], "samp", ring[d])

    def w_local(k):
        return pltpu.make_async_copy(wbuf.at[k], wout.at[:, cols(y, k)], wl_sem.at[k])

    def each(count, body):
        lax.fori_loop(0, count, lambda i, c: (body(i), c)[1], 0)

    def start_local(k):
        own_copy(k).start()
        w_load(k).start()
        e_load(k).start()

    for k in range(V_SLOTS):
        for copy in v_load(k, k):
            copy.start()

    barrier = pltpu.get_barrier_semaphore()
    for o in range(1, ns):
        pl.semaphore_signal(barrier, inc=1, device_id={"samp": lax.rem(y + o, ns)}, device_id_type=MESH)
    for o in range(1, nf):
        pl.semaphore_signal(barrier, inc=1, device_id={"feat": lax.rem(f + o, nf)}, device_id_type=MESH)
    pl.semaphore_wait(barrier, ns - 1 + nf - 1)

    def start_relay(i):
        for d in range(2):
            relay_copy(d, i).start()

    each(half, start_relay)

    def v_step(k, acc):
        slot = lax.rem(k, V_SLOTS)
        for copy in v_load(k, slot):
            copy.wait()
        low = vw[slot].astype(jnp.bfloat16)
        acc = acc + lax.dot_general(low, vx[slot], NT, preferred_element_type=jnp.float32)

        @pl.when(k + V_SLOTS < v_steps)
        def _():
            for copy in v_load(k + V_SLOTS, slot):
                copy.start()

        return acc

    first = lax.fori_loop(0, v_steps, v_step, jnp.zeros((targets, rows), jnp.float32))
    each(CHUNKS, start_local)

    def a_copy(t, o, place):
        to = lax.rem(y + o, ns)
        return remote(usend.at[t, to], rsbuf.at[t, place], a_s.at[t, o - 1], a_r.at[t, o - 1], "samp", to)

    def b_copy(t, o, place):
        return remote(agbuf.at[t, f], agbuf.at[t, place], b_s.at[t, o - 1], b_r.at[t, o - 1], "feat", lax.rem(f + o, nf))

    def c_copy(t, o, place):
        return remote(rbuf.at[t, y], rbuf.at[t, place], c_s.at[t, o - 1], c_r.at[t, o - 1], "samp", lax.rem(y + o, ns))

    def start_a(t, u):
        for s in range(ns):
            usend[t, s] = u[:, s * rows:(s + 1) * rows]
        for o in range(1, ns):
            a_copy(t, o, y).start()
        rsbuf[t, y] = usend[t, y]

    def finish_a(t):
        for o in range(1, ns):
            a_copy(t, o, lax.rem(y + ns - o, ns)).wait_recv()
        total = rsbuf[t, 0]
        for s in range(1, ns):
            total = total + rsbuf[t, s]
        return total

    def sum_blocks(t, term):
        agbuf[t, f] = term.astype(jnp.bfloat16)
        for o in range(1, nf):
            b_copy(t, o, f).start()
        for o in range(1, nf):
            b_copy(t, o, lax.rem(f + nf - o, nf)).wait_recv()
        total = agbuf[t, 0].astype(jnp.float32)
        for j in range(1, nf):
            total = total + agbuf[t, j].astype(jnp.float32)
        return total

    def start_c(t):
        rbuf[t, y] = rstate[...].astype(jnp.bfloat16)
        for o in range(1, ns):
            c_copy(t, o, y).start()

    def finish_c(t):
        for o in range(1, ns):
            c_copy(t, o, lax.rem(y + ns - o, ns)).wait_recv()
        return jnp.concatenate([rbuf[t, s] for s in range(ns)], axis=1)

    rstate[...] = yt_ref[...] - sum_blocks(0, first)
    start_c(0)

    def start_direct(k):
        for d in range(2):
            direct_copy(d, k, y).start()

    each(CHUNKS, start_direct)

    def start_forward(i):
        for d in range(2):
            relay_copy(d, i).wait_recv()
            forward_copy(d, i, ring[1 - d]).start()

    each(half, start_forward)

    def sweep_chunk(k, resid, u):
        for s in range(chunk // sub):
            part = pl.ds(s * sub, sub)
            x_part = xbuf[k, :, part]
            grad = jnp.dot(resid, x_part, preferred_element_type=jnp.float32) * inv
            w_part = wbuf[k, :, part]
            delta = ebuf[k, :, part] * (grad - ridge * w_part)
            wbuf[k, :, part] = w_part + COMBINE_WEIGHT * delta
            u = u + lax.dot_general(delta.astype(jnp.bfloat16), x_part, NT, preferred_element_type=jnp.float32)
        return u

    zero = jnp.zeros((targets, samples), jnp.float32)

    def arriving(i, carry):
        resid, u = carry
        for d in range(2):
            k = 2 * i + d
            own_copy(k).wait()
            w_load(k).wait()
            e_load(k).wait()
            for e in range(2):
                direct_copy(e, k, ring[1 - e]).wait_recv()
            forward_copy(d, i, far).wait_recv()
            u = sweep_chunk(k, resid, u)
        return resid, u

    def staying(k, carry):
        resid, u = carry
        return resid, sweep_chunk(k, resid, u)

    def send_w(k):
        for d in range(2):
            wd_copy(d, k, y).start()
        w_local(k).start()

    def leaving(k, carry):
        resid, u = carry
        u = sweep_chunk(k, resid, u)

        @pl.when(k > 0)
        def _():
            send_w(k - 1)

        return resid, u

    for t in range(SWEEPS):
        resid = finish_c(t)
        if t == 0:
            _, u = lax.fori_loop(0, half, arriving, (resid, zero))
        elif t < SWEEPS - 1:
            _, u = lax.fori_loop(0, CHUNKS, staying, (resid, zero))
        else:
            _, u = lax.fori_loop(0, CHUNKS, leaving, (resid, zero))
        start_a(t, u)
        if t < SWEEPS - 1:
            rstate[...] = rstate[...] - COMBINE_WEIGHT * sum_blocks(t + 1, finish_a(t))
            start_c(t + 1)

    send_w(CHUNKS - 1)

    def start_wf(i):
        for d in range(2):
            k = 2 * i + d
            for e in range(2):
                wd_copy(e, k, ring[1 - e]).wait_recv()
            wf_copy(d, i, ring[1 - d]).start()

    def start_wf_pair(i):
        start_wf(i)

    each(half, start_wf_pair)
    rout[...] = rstate[...] - COMBINE_WEIGHT * sum_blocks(SWEEPS, finish_a(SWEEPS - 1))

    def finish_half(i):
        for d in range(2):
            relay_copy(d, i).wait_send()
            forward_copy(d, i, ring[1 - d]).wait_send()
            wf_copy(d, i, far).wait_recv()
            wf_copy(d, i, ring[1 - d]).wait_send()

    def finish_full(k):
        for d in range(2):
            direct_copy(d, k, y).wait_send()
            wd_copy(d, k, y).wait_send()
        w_local(k).wait()

    each(CHUNKS, finish_full)
    each(half, finish_half)
    for t in range(SWEEPS):
        for o in range(1, ns):
            a_copy(t, o, y).wait_send()
            c_copy(t, o, y).wait_send()
    for t in range(SWEEPS + 1):
        for o in range(1, nf):
            b_copy(t, o, f).wait_send()


def solution(mesh):
    ns, nf = mesh.shape["samp"], mesh.shape["feat"]

    def local_solve(x_loc, w_loc, y_loc, eta_loc):
        rows, feat_len = x_loc.shape
        targets = w_loc.shape[1]
        samples = rows * ns
        chunk = feat_len // ns // CHUNKS
        half = CHUNKS // 2
        dma = pltpu.SemaphoreType.DMA
        hbm = pl.BlockSpec(memory_space=pl.ANY)
        vmem = pl.BlockSpec(memory_space=pltpu.VMEM)
        small = feat_len * targets
        w_out, r_out = pl.pallas_call(
            functools.partial(kernel, ns, nf),
            out_shape=(jax.ShapeDtypeStruct((targets, feat_len), jnp.float32), jax.ShapeDtypeStruct((targets, rows), jnp.float32)),
            in_specs=[hbm, hbm, vmem, hbm],
            out_specs=(hbm, vmem),
            scratch_shapes=[
                pltpu.VMEM((CHUNKS, samples, chunk), jnp.bfloat16),
                pltpu.VMEM((2, half, rows, chunk), jnp.bfloat16),
                pltpu.VMEM((CHUNKS, targets, chunk), jnp.float32),
                pltpu.VMEM((CHUNKS, 1, chunk), jnp.float32),
                pltpu.VMEM((V_SLOTS, rows, chunk), jnp.bfloat16),
                pltpu.VMEM((V_SLOTS, targets, chunk), jnp.float32),
                pltpu.VMEM((SWEEPS, ns, targets, rows), jnp.float32),
                pltpu.VMEM((SWEEPS, ns, targets, rows), jnp.float32),
                pltpu.VMEM((SWEEPS + 1, nf, targets, rows), jnp.bfloat16),
                pltpu.VMEM((SWEEPS, ns, targets, rows), jnp.bfloat16),
                pltpu.VMEM((targets, rows), jnp.float32),
                dma((CHUNKS,)), dma((CHUNKS,)), dma((CHUNKS,)), dma((2, V_SLOTS)),
                dma((2, half)), dma((2, half)), dma((2, CHUNKS)), dma((2, CHUNKS)), dma((2, half)), dma((2, half)),
                dma((SWEEPS, ns - 1)), dma((SWEEPS, ns - 1)),
                dma((SWEEPS + 1, nf - 1)), dma((SWEEPS + 1, nf - 1)),
                dma((SWEEPS, ns - 1)), dma((SWEEPS, ns - 1)),
                dma((CHUNKS,)), dma((2, CHUNKS)), dma((2, CHUNKS)), dma((2, half)), dma((2, half)),
            ],
            compiler_params=pltpu.CompilerParams(collective_id=0, has_side_effects=True, vmem_limit_bytes=64 * 1024 * 1024 - 256 * 1024),
            cost_estimate=pl.CostEstimate(flops=2 * rows * small * (2 * SWEEPS + 1), bytes_accessed=8 * small + 4 * rows * feat_len,
                                          transcendentals=0),
            name="ridge_sweeps",
        )(x_loc, w_loc.T, y_loc.T, eta_loc.reshape(1, feat_len))
        return w_out.T, r_out.T

    return jax.shard_map(
        local_solve,
        mesh=mesh,
        in_specs=(P(("prob", "samp"), "feat"), P(("prob", "feat"), None), P(("prob", "samp"), None), P(("prob", "feat"))),
        out_specs=(P(("prob", "feat"), None), P(("prob", "samp"), None)),
        check_vma=False,
    )
```

time: 1520 us -> 600 us (0.39)
  waiting for transfers between devices: 1140 us -> 0 us
  Pallas kernels: 0 us -> 587 us
  matrix products: 201 us -> 0 us
  blocking collectives: 115 us -> 0 us
  other arithmetic: 48.2 us -> 0 us
    psum x4 -> x0, waiting for transfers between devices: 1140 us -> none  [local_solve(): gradient = lax.psum(part_grad, 'samp') / samples]
    pallas_call x0 -> x1, Pallas kernels: none -> 587 us  [local_solve(): pl.pallas_call(functools.partial(kernel, ns, nf), out_shape=(jax.ShapeDty...]
    dot_general x9 -> x0, matrix products: 201 us -> none  [the longest x4 103 us: local_solve(): jnp.dot(x_loc, delta.astype(jnp.bfloat16), preferred_element_type=jnp.flo...]
    psum x5 -> x0, blocking collectives: 115 us -> none  [the longest x4 90.9 us: local_solve(): lax.psum(update.astype(jnp.bfloat16).astype(jnp.float32), 'feat')]
    add x2 -> x0, other arithmetic: 47.6 us -> none  [local_solve(): weights = weights + COMBINE_WEIGHT * delta]
  transfers between devices with their start and end apart: 4 -> 0, of which waited for: 4 -> 0; matrix products, arithmetic and copies ran while one was open for 2% -> 0% of each run, Pallas kernels for 0% -> 0%
where the time goes in v1:
time: 600 us
  Pallas kernels  587 us (98%)
  local copies, waits for them, and re-layouts  12 us (2%)
    pallas_call x1, Pallas kernels, local_solve(): pl.pallas_call(functools.partial(kernel, ns, nf), out_shape=(jax.ShapeDty...  587 us
    unnamed x4, local copies, waits for them, and re-layouts  12 us

profile of v1, /device:TPU:97, one launch (start us, length us, event | category | flops | bytes accessed | tf_op | source)
XLA Modules:
  0.0 600.0 jit_solution(15796456358438640259)
XLA Ops:
  0.6 587.3 %ridge_sweeps.1 = (f32[32,131072]{1,0:T(8,128)}, f32[32,128]{1,0:T(8,128)}) custom-call(bf16[128,131072]{1,0:T(8,128)(2,1)} %x_hbm.1, f32[32,131072]{1,0:T(8,128)} %bitcast.5, f32[32,128]{1,0:T(8,128)} %bitcast.8, f32[1,131072]{1,0:T(1,128)} %bitcast.7), custom_call_target="tpu_custom_call" | custom-call | flops 9663676416 | bytes 100663296 | tf_op jit(solution)/shard_map/ridge_sweeps/pallas_call | solution.py:297
  587.9 0.0 copy-start
  587.9 11.4 %copy.8 = f32[131072,32]{0,1:T(8,128)} copy(f32[131072,32]{0,1:T(8,128)} %bitcast.6) | data formatting | bytes 33554432
  599.4 0.0 copy-done
  599.4 0.6 copy.9
Async XLA Ops:
  587.9 11.4 %copy-start = (f32[32,128]{1,0:T(8,128)S(1)}, f32[32,128]{1,0:T(8,128)}, u32[]{:S(2)}) copy-start(f32[32,128]{1,0:T(8,128)} %get-tuple-element.5) | copy-start | bytes 49156

commit v2 on v1

--- a/solution.py
+++ b/solution.py
@@ -12,14 +12,19 @@
 RIDGE_SCALE = 0.1
 CHUNKS = 16
 SUB = 512
+STREAM = 0.5
 V_SLOTS = 4
 MESH = pl.DeviceIdType.MESH
 NT = (((1,), (1,)), ((), ()))
 
 
-def kernel(ns, nf, x_hbm, wt_hbm, yt_ref, eta_hbm, wout, rout, xbuf, relay, wbuf, ebuf, vx, vw, usend, rsbuf, agbuf, rbuf, rstate,
+def far_first(count):
+    return sorted(range(1, count), key=lambda o: -min(o, count - o))
+
+
+def kernel(ns, nf, x_hbm, wt_hbm, yt_ref, eta_hbm, wout, rout, xbuf, relay, ebuf, vx, vw, usend, rsbuf, agbuf, rbuf, rstate, ucol, urow,
            own_sem, w_sem, e_sem, v_sem, rel_s, rel_r, dir_s, dir_r, fwd_s, fwd_r, a_s, a_r, b_s, b_r, c_s, c_r,
-           wl_sem, wd_s, wd_r, wf_s, wf_r):
+           wd_s, wd_r, wf_s, wf_r):
     y, f = lax.axis_index("samp"), lax.axis_index("feat")
     rows, feat_len = x_hbm.shape
     targets = wt_hbm.shape[0]
@@ -47,7 +52,7 @@
         return pltpu.make_async_copy(x_hbm.at[:, cols(y, k)], xbuf.at[k, rows_of(y), :], own_sem.at[k])
 
     def w_load(k):
-        return pltpu.make_async_copy(wt_hbm.at[:, cols(y, k)], wbuf.at[k], w_sem.at[k])
+        return pltpu.make_async_copy(wt_hbm.at[:, cols(y, k)], wout.at[:, cols(y, k)], w_sem.at[k])
 
     def e_load(k):
         return pltpu.make_async_copy(eta_hbm.at[:, cols(y, k)], ebuf.at[k], e_sem.at[k])
@@ -71,14 +76,11 @@
         return remote(relay.at[d, i], xbuf.at[2 * i + d, rows_of(place), :], fwd_s.at[d, i], fwd_r.at[d, i], "samp", ring[d])
 
     def wd_copy(d, k, owner):
-        return remote(wbuf.at[k], wout.at[:, cols(owner, k)], wd_s.at[d, k], wd_r.at[d, k], "samp", ring[d])
+        return remote(wout.at[:, cols(y, k)], wout.at[:, cols(owner, k)], wd_s.at[d, k], wd_r.at[d, k], "samp", ring[d])
 
     def wf_copy(d, i, owner):
         part = wout.at[:, cols(owner, 2 * i + d)]
         return remote(part, part, wf_s.at[d, i], wf_r.at[d, i], "samp", ring[d])
-
-    def w_local(k):
-        return pltpu.make_async_copy(wbuf.at[k], wout.at[:, cols(y, k)], wl_sem.at[k])
 
     def each(count, body):
         lax.fori_loop(0, count, lambda i, c: (body(i), c)[1], 0)
@@ -132,10 +134,10 @@
     def c_copy(t, o, place):
         return remote(rbuf.at[t, y], rbuf.at[t, place], c_s.at[t, o - 1], c_r.at[t, o - 1], "samp", lax.rem(y + o, ns))
 
-    def start_a(t, u):
+    def start_a(t):
         for s in range(ns):
-            usend[t, s] = u[:, s * rows:(s + 1) * rows]
-        for o in range(1, ns):
+            usend[t, s] = ucol[s * rows:(s + 1) * rows, :].T + urow[:, s * rows:(s + 1) * rows]
+        for o in far_first(ns):
             a_copy(t, o, y).start()
         rsbuf[t, y] = usend[t, y]
 
@@ -149,7 +151,7 @@
 
     def sum_blocks(t, term):
         agbuf[t, f] = term.astype(jnp.bfloat16)
-        for o in range(1, nf):
+        for o in far_first(nf):
             b_copy(t, o, f).start()
         for o in range(1, nf):
             b_copy(t, o, lax.rem(f + nf - o, nf)).wait_recv()
@@ -160,7 +162,7 @@
 
     def start_c(t):
         rbuf[t, y] = rstate[...].astype(jnp.bfloat16)
-        for o in range(1, ns):
+        for o in far_first(ns):
             c_copy(t, o, y).start()
 
     def finish_c(t):
@@ -184,21 +186,30 @@
 
     each(half, start_forward)
 
-    def sweep_chunk(k, resid, u):
-        for s in range(chunk // sub):
+    def sweep_chunk(k, resid):
+        parts = chunk // sub
+        col, row = None, None
+        for s in range(parts):
             part = pl.ds(s * sub, sub)
             x_part = xbuf[k, :, part]
             grad = jnp.dot(resid, x_part, preferred_element_type=jnp.float32) * inv
-            w_part = wbuf[k, :, part]
+            place = pl.ds(pl.multiple_of(y * own + k * chunk + s * sub, sub), sub)
+            w_part = wout[:, place]
             delta = ebuf[k, :, part] * (grad - ridge * w_part)
-            wbuf[k, :, part] = w_part + COMBINE_WEIGHT * delta
-            u = u + lax.dot_general(delta.astype(jnp.bfloat16), x_part, NT, preferred_element_type=jnp.float32)
-        return u
-
-    zero = jnp.zeros((targets, samples), jnp.float32)
-
-    def arriving(i, carry):
-        resid, u = carry
+            wout[:, place] = w_part + COMBINE_WEIGHT * delta
+            low = delta.astype(jnp.bfloat16)
+            if s < STREAM * parts:
+                term = lax.dot_general(x_part, low, NT, preferred_element_type=jnp.float32)
+                col = term if col is None else col + term
+            else:
+                term = lax.dot_general(low, x_part, NT, preferred_element_type=jnp.float32)
+                row = term if row is None else row + term
+        if col is not None:
+            ucol[...] += col
+        if row is not None:
+            urow[...] += row
+
+    def arriving(i):
         for d in range(2):
             k = 2 * i + d
             own_copy(k).wait()
@@ -207,37 +218,33 @@
             for e in range(2):
                 direct_copy(e, k, ring[1 - e]).wait_recv()
             forward_copy(d, i, far).wait_recv()
-            u = sweep_chunk(k, resid, u)
-        return resid, u
-
-    def staying(k, carry):
-        resid, u = carry
-        return resid, sweep_chunk(k, resid, u)
+            sweep_chunk(k, resid)
+
+    def staying(k):
+        sweep_chunk(k, resid)
 
     def send_w(k):
         for d in range(2):
             wd_copy(d, k, y).start()
-        w_local(k).start()
-
-    def leaving(k, carry):
-        resid, u = carry
-        u = sweep_chunk(k, resid, u)
+
+    def leaving(k):
+        sweep_chunk(k, resid)
 
         @pl.when(k > 0)
         def _():
             send_w(k - 1)
 
-        return resid, u
-
     for t in range(SWEEPS):
         resid = finish_c(t)
+        ucol[...] = jnp.zeros_like(ucol)
+        urow[...] = jnp.zeros_like(urow)
         if t == 0:
-            _, u = lax.fori_loop(0, half, arriving, (resid, zero))
+            each(half, arriving)
         elif t < SWEEPS - 1:
-            _, u = lax.fori_loop(0, CHUNKS, staying, (resid, zero))
+            each(CHUNKS, staying)
         else:
-            _, u = lax.fori_loop(0, CHUNKS, leaving, (resid, zero))
-        start_a(t, u)
+            each(CHUNKS, leaving)
+        start_a(t)
         if t < SWEEPS - 1:
             rstate[...] = rstate[...] - COMBINE_WEIGHT * sum_blocks(t + 1, finish_a(t))
             start_c(t + 1)
@@ -268,7 +275,6 @@
         for d in range(2):
             direct_copy(d, k, y).wait_send()
             wd_copy(d, k, y).wait_send()
-        w_local(k).wait()
 
     each(CHUNKS, finish_full)
     each(half, finish_half)
@@ -296,13 +302,12 @@
         small = feat_len * targets
         w_out, r_out = pl.pallas_call(
             functools.partial(kernel, ns, nf),
-            out_shape=(jax.ShapeDtypeStruct((targets, feat_len), jnp.float32), jax.ShapeDtypeStruct((targets, rows), jnp.float32)),
+            out_shape=(pltpu.VMEM((targets, feat_len), jnp.float32), pltpu.VMEM((targets, rows), jnp.float32)),
             in_specs=[hbm, hbm, vmem, hbm],
-            out_specs=(hbm, vmem),
+            out_specs=(vmem, vmem),
             scratch_shapes=[
                 pltpu.VMEM((CHUNKS, samples, chunk), jnp.bfloat16),
                 pltpu.VMEM((2, half, rows, chunk), jnp.bfloat16),
-                pltpu.VMEM((CHUNKS, targets, chunk), jnp.float32),
                 pltpu.VMEM((CHUNKS, 1, chunk), jnp.float32),
                 pltpu.VMEM((V_SLOTS, rows, chunk), jnp.bfloat16),
                 pltpu.VMEM((V_SLOTS, targets, chunk), jnp.float32),
@@ -311,14 +316,16 @@
                 pltpu.VMEM((SWEEPS + 1, nf, targets, rows), jnp.bfloat16),
                 pltpu.VMEM((SWEEPS, ns, targets, rows), jnp.bfloat16),
                 pltpu.VMEM((targets, rows), jnp.float32),
+                pltpu.VMEM((samples, targets), jnp.float32),
+                pltpu.VMEM((targets, samples), jnp.float32),
                 dma((CHUNKS,)), dma((CHUNKS,)), dma((CHUNKS,)), dma((2, V_SLOTS)),
                 dma((2, half)), dma((2, half)), dma((2, CHUNKS)), dma((2, CHUNKS)), dma((2, half)), dma((2, half)),
                 dma((SWEEPS, ns - 1)), dma((SWEEPS, ns - 1)),
                 dma((SWEEPS + 1, nf - 1)), dma((SWEEPS + 1, nf - 1)),
                 dma((SWEEPS, ns - 1)), dma((SWEEPS, ns - 1)),
-                dma((CHUNKS,)), dma((2, CHUNKS)), dma((2, CHUNKS)), dma((2, half)), dma((2, half)),
+                dma((2, CHUNKS)), dma((2, CHUNKS)), dma((2, half)), dma((2, half)),
             ],
-            compiler_params=pltpu.CompilerParams(collective_id=0, has_side_effects=True, vmem_limit_bytes=64 * 1024 * 1024 - 256 * 1024),
+            compiler_params=pltpu.CompilerParams(collective_id=0, has_side_effects=True, vmem_limit_bytes=47 * 1024 * 1024),
             cost_estimate=pl.CostEstimate(flops=2 * rows * small * (2 * SWEEPS + 1), bytes_accessed=8 * small + 4 * rows * feat_len,
                                           transcendentals=0),
             name="ridge_sweeps",

time: 600 us -> 591 us (0.985)
    unnamed x4 -> x2, local copies, waits for them, and re-layouts: 12 us -> 6.77 us
where the time goes in v2:
time: 591 us
  Pallas kernels  583 us (99%)
  local copies, waits for them, and re-layouts  6.77 us (1%)
    pallas_call x1, Pallas kernels, local_solve(): pl.pallas_call(functools.partial(kernel, ns, nf), out_shape=(pltpu.VMEM((...  583 us

profile of v2, /device:TPU:97, one launch (start us, length us, event | category | flops | bytes accessed | tf_op | source)
XLA Modules:
  0.0 590.6 jit_solution(12656185845621895707)
XLA Ops:
  0.6 583.2 %ridge_sweeps.1 = (f32[32,131072]{1,0:T(8,128)S(1)}, f32[32,128]{1,0:T(8,128)S(1)}) custom-call(bf16[128,131072]{1,0:T(8,128)(2,1)} %x_hbm.1, f32[32,131072]{1,0:T(8,128)} %bitcast.7, f32[32,128]{1,0:T(8,128)} %bitcast.9, f32[1,131072]{1,0:T(1,128)} %bitcast.8), custom_call_target="tpu_custom_call" | custom-call | flops 9663676416 | bytes 100663296 | tf_op jit(solution)/shard_map/ridge_sweeps/pallas_call | solution.py:303
  583.8 6.2 %copy.8 = f32[131072,32]{0,1:T(8,128)} copy(f32[131072,32]{0,1:T(8,128)S(1)} %bitcast.5) | data formatting | bytes 33554432
  590.0 0.6 copy.9

commit v3 on v2

--- a/solution.py
+++ b/solution.py
@@ -13,7 +13,7 @@
 CHUNKS = 16
 SUB = 512
 STREAM = 0.5
-V_SLOTS = 4
+V_SLOTS = 3
 MESH = pl.DeviceIdType.MESH
 NT = (((1,), (1,)), ((), ()))
 
@@ -22,7 +22,7 @@
     return sorted(range(1, count), key=lambda o: -min(o, count - o))
 
 
-def kernel(ns, nf, x_hbm, wt_hbm, yt_ref, eta_hbm, wout, rout, xbuf, relay, ebuf, vx, vw, usend, rsbuf, agbuf, rbuf, rstate, ucol, urow,
+def kernel(ns, nf, x_hbm, wt_hbm, yt_ref, eta_hbm, wout, rout, xbuf, relay, dbuf, ebuf, vx, vw, usend, rsbuf, agbuf, rbuf, rstate, ucol, urow,
            own_sem, w_sem, e_sem, v_sem, rel_s, rel_r, dir_s, dir_r, fwd_s, fwd_r, a_s, a_r, b_s, b_r, c_s, c_r,
            wd_s, wd_r, wf_s, wf_r):
     y, f = lax.axis_index("samp"), lax.axis_index("feat")
@@ -41,15 +41,15 @@
     def cols(owner, k):
         return pl.ds(pl.multiple_of(owner * own + k * chunk, chunk), chunk)
 
-    def rows_of(s):
-        return pl.ds(pl.multiple_of(s * rows, rows), rows)
+    def rows_of(o):
+        return pl.ds(o * rows, rows)
 
     def remote(src, dst, send, recv, axis, dev):
         return pltpu.make_async_remote_copy(src_ref=src, dst_ref=dst, send_sem=send, recv_sem=recv,
                                             device_id={axis: dev}, device_id_type=MESH)
 
     def own_copy(k):
-        return pltpu.make_async_copy(x_hbm.at[:, cols(y, k)], xbuf.at[k, rows_of(y), :], own_sem.at[k])
+        return pltpu.make_async_copy(x_hbm.at[:, cols(y, k)], xbuf.at[k, rows_of(0), :], own_sem.at[k])
 
     def w_load(k):
         return pltpu.make_async_copy(wt_hbm.at[:, cols(y, k)], wout.at[:, cols(y, k)], w_sem.at[k])
@@ -69,11 +69,11 @@
     def relay_copy(d, i):
         return remote(x_hbm.at[:, cols(far, 2 * i + d)], relay.at[d, i], rel_s.at[d, i], rel_r.at[d, i], "samp", ring[d])
 
-    def direct_copy(d, k, place):
-        return remote(x_hbm.at[:, cols(ring[d], k)], xbuf.at[k, rows_of(place), :], dir_s.at[d, k], dir_r.at[d, k], "samp", ring[d])
-
-    def forward_copy(d, i, place):
-        return remote(relay.at[d, i], xbuf.at[2 * i + d, rows_of(place), :], fwd_s.at[d, i], fwd_r.at[d, i], "samp", ring[d])
+    def direct_copy(d, k):
+        return remote(x_hbm.at[:, cols(ring[d], k)], xbuf.at[k, rows_of((ns - 1, 1)[d]), :], dir_s.at[d, k], dir_r.at[d, k], "samp", ring[d])
+
+    def forward_copy(d, i):
+        return remote(relay.at[d, i], xbuf.at[2 * i + d, rows_of(2), :], fwd_s.at[d, i], fwd_r.at[d, i], "samp", ring[d])
 
     def wd_copy(d, k, owner):
         return remote(wout.at[:, cols(y, k)], wout.at[:, cols(owner, k)], wd_s.at[d, k], wd_r.at[d, k], "samp", ring[d])
@@ -124,29 +124,26 @@
     first = lax.fori_loop(0, v_steps, v_step, jnp.zeros((targets, rows), jnp.float32))
     each(CHUNKS, start_local)
 
-    def a_copy(t, o, place):
-        to = lax.rem(y + o, ns)
-        return remote(usend.at[t, to], rsbuf.at[t, place], a_s.at[t, o - 1], a_r.at[t, o - 1], "samp", to)
+    def a_copy(t, o):
+        return remote(usend.at[t, o], rsbuf.at[t, ns - o], a_s.at[t, o - 1], a_r.at[t, o - 1], "samp", lax.rem(y + o, ns))
 
     def b_copy(t, o, place):
         return remote(agbuf.at[t, f], agbuf.at[t, place], b_s.at[t, o - 1], b_r.at[t, o - 1], "feat", lax.rem(f + o, nf))
 
-    def c_copy(t, o, place):
-        return remote(rbuf.at[t, y], rbuf.at[t, place], c_s.at[t, o - 1], c_r.at[t, o - 1], "samp", lax.rem(y + o, ns))
+    def c_copy(t, o):
+        return remote(rbuf.at[t, 0], rbuf.at[t, ns - o], c_s.at[t, o - 1], c_r.at[t, o - 1], "samp", lax.rem(y + o, ns))
 
     def start_a(t):
-        for s in range(ns):
-            usend[t, s] = ucol[s * rows:(s + 1) * rows, :].T + urow[:, s * rows:(s + 1) * rows]
+        for o in range(1, ns):
+            usend[t, o] = ucol[(o - 1) * rows:o * rows, :].T + urow[:, (o - 1) * rows:o * rows]
         for o in far_first(ns):
-            a_copy(t, o, y).start()
-        rsbuf[t, y] = usend[t, y]
-
-    def finish_a(t):
-        for o in range(1, ns):
-            a_copy(t, o, lax.rem(y + ns - o, ns)).wait_recv()
-        total = rsbuf[t, 0]
-        for s in range(1, ns):
-            total = total + rsbuf[t, s]
+            a_copy(t, o).start()
+
+    def finish_a(t, total):
+        for o in range(1, ns):
+            a_copy(t, o).wait_recv()
+        for o in range(1, ns):
+            total = total + rsbuf[t, o]
         return total
 
     def sum_blocks(t, term):
@@ -161,43 +158,49 @@
         return total
 
     def start_c(t):
-        rbuf[t, y] = rstate[...].astype(jnp.bfloat16)
+        rbuf[t, 0] = rstate[...].astype(jnp.bfloat16)
         for o in far_first(ns):
-            c_copy(t, o, y).start()
+            c_copy(t, o).start()
 
     def finish_c(t):
         for o in range(1, ns):
-            c_copy(t, o, lax.rem(y + ns - o, ns)).wait_recv()
-        return jnp.concatenate([rbuf[t, s] for s in range(ns)], axis=1)
+            c_copy(t, o).wait_recv()
+        return jnp.concatenate([rbuf[t, o] for o in range(ns)], axis=1)
 
     rstate[...] = yt_ref[...] - sum_blocks(0, first)
     start_c(0)
 
     def start_direct(k):
         for d in range(2):
-            direct_copy(d, k, y).start()
+            direct_copy(d, k).start()
 
     each(CHUNKS, start_direct)
 
     def start_forward(i):
         for d in range(2):
             relay_copy(d, i).wait_recv()
-            forward_copy(d, i, ring[1 - d]).start()
+            forward_copy(d, i).start()
 
     each(half, start_forward)
 
-    def sweep_chunk(k, resid):
-        parts = chunk // sub
+    parts = chunk // sub
+
+    def advance(k, s, resid):
+        part = pl.ds(s * sub, sub)
+        grad = jnp.dot(resid, xbuf[k, :, part], preferred_element_type=jnp.float32) * inv
+        place = pl.ds(pl.multiple_of(y * own + k * chunk + s * sub, sub), sub)
+        w_part = wout[:, place]
+        delta = ebuf[k, :, part] * (grad - ridge * w_part)
+        wout[:, place] = w_part + COMBINE_WEIGHT * delta
+        low = delta.astype(jnp.bfloat16)
+        dbuf[k, :, part] = low
+        return low
+
+    def other_rows(k, low_of):
         col, row = None, None
         for s in range(parts):
-            part = pl.ds(s * sub, sub)
-            x_part = xbuf[k, :, part]
-            grad = jnp.dot(resid, x_part, preferred_element_type=jnp.float32) * inv
-            place = pl.ds(pl.multiple_of(y * own + k * chunk + s * sub, sub), sub)
-            w_part = wout[:, place]
-            delta = ebuf[k, :, part] * (grad - ridge * w_part)
-            wout[:, place] = w_part + COMBINE_WEIGHT * delta
-            low = delta.astype(jnp.bfloat16)
+            low = low_of(s)
+            x_part = xbuf[k, rows:, pl.ds(s * sub, sub)]
             if s < STREAM * parts:
                 term = lax.dot_general(x_part, low, NT, preferred_element_type=jnp.float32)
                 col = term if col is None else col + term
@@ -209,6 +212,12 @@
         if row is not None:
             urow[...] += row
 
+    def sweep_chunk(k, resid):
+        other_rows(k, lambda s: advance(k, s, resid))
+
+    def own_rows(k, acc):
+        return acc + lax.dot_general(xbuf[k, :rows, :], dbuf[k], NT, preferred_element_type=jnp.float32)
+
     def arriving(i):
         for d in range(2):
             k = 2 * i + d
@@ -216,19 +225,24 @@
             w_load(k).wait()
             e_load(k).wait()
             for e in range(2):
-                direct_copy(e, k, ring[1 - e]).wait_recv()
-            forward_copy(d, i, far).wait_recv()
+                direct_copy(e, k).wait_recv()
+            forward_copy(d, i).wait_recv()
             sweep_chunk(k, resid)
 
+    def from_store(k):
+        other_rows(k, lambda s: dbuf[k, :, pl.ds(s * sub, sub)])
+
     def staying(k):
-        sweep_chunk(k, resid)
+        for s in range(parts):
+            advance(k, s, resid)
 
     def send_w(k):
         for d in range(2):
             wd_copy(d, k, y).start()
 
     def leaving(k):
-        sweep_chunk(k, resid)
+        for s in range(parts):
+            advance(k, s, resid)
 
         @pl.when(k > 0)
         def _():
@@ -242,14 +256,16 @@
             each(half, arriving)
         elif t < SWEEPS - 1:
             each(CHUNKS, staying)
+            each(CHUNKS, from_store)
         else:
             each(CHUNKS, leaving)
+            send_w(CHUNKS - 1)
+            each(CHUNKS, from_store)
         start_a(t)
+        mine = lax.fori_loop(0, CHUNKS, own_rows, jnp.zeros((rows, targets), jnp.float32)).T
         if t < SWEEPS - 1:
-            rstate[...] = rstate[...] - COMBINE_WEIGHT * sum_blocks(t + 1, finish_a(t))
+            rstate[...] = rstate[...] - COMBINE_WEIGHT * sum_blocks(t + 1, finish_a(t, mine))
             start_c(t + 1)
-
-    send_w(CHUNKS - 1)
 
     def start_wf(i):
         for d in range(2):
@@ -262,26 +278,26 @@
         start_wf(i)
 
     each(half, start_wf_pair)
-    rout[...] = rstate[...] - COMBINE_WEIGHT * sum_blocks(SWEEPS, finish_a(SWEEPS - 1))
+    rout[...] = rstate[...] - COMBINE_WEIGHT * sum_blocks(SWEEPS, finish_a(SWEEPS - 1, mine))
 
     def finish_half(i):
         for d in range(2):
             relay_copy(d, i).wait_send()
-            forward_copy(d, i, ring[1 - d]).wait_send()
+            forward_copy(d, i).wait_send()
             wf_copy(d, i, far).wait_recv()
             wf_copy(d, i, ring[1 - d]).wait_send()
 
     def finish_full(k):
         for d in range(2):
-            direct_copy(d, k, y).wait_send()
+            direct_copy(d, k).wait_send()
             wd_copy(d, k, y).wait_send()
 
     each(CHUNKS, finish_full)
     each(half, finish_half)
     for t in range(SWEEPS):
         for o in range(1, ns):
-            a_copy(t, o, y).wait_send()
-            c_copy(t, o, y).wait_send()
+            a_copy(t, o).wait_send()
+            c_copy(t, o).wait_send()
     for t in range(SWEEPS + 1):
         for o in range(1, nf):
             b_copy(t, o, f).wait_send()
@@ -308,6 +324,7 @@
             scratch_shapes=[
                 pltpu.VMEM((CHUNKS, samples, chunk), jnp.bfloat16),
                 pltpu.VMEM((2, half, rows, chunk), jnp.bfloat16),
+                pltpu.VMEM((CHUNKS, targets, chunk), jnp.bfloat16),
                 pltpu.VMEM((CHUNKS, 1, chunk), jnp.float32),
                 pltpu.VMEM((V_SLOTS, rows, chunk), jnp.bfloat16),
                 pltpu.VMEM((V_SLOTS, targets, chunk), jnp.float32),
@@ -316,8 +333,8 @@
                 pltpu.VMEM((SWEEPS + 1, nf, targets, rows), jnp.bfloat16),
                 pltpu.VMEM((SWEEPS, ns, targets, rows), jnp.bfloat16),
                 pltpu.VMEM((targets, rows), jnp.float32),
-                pltpu.VMEM((samples, targets), jnp.float32),
-                pltpu.VMEM((targets, samples), jnp.float32),
+                pltpu.VMEM((samples - rows, targets), jnp.float32),
+                pltpu.VMEM((targets, samples - rows), jnp.float32),
                 dma((CHUNKS,)), dma((CHUNKS,)), dma((CHUNKS,)), dma((2, V_SLOTS)),
                 dma((2, half)), dma((2, half)), dma((2, CHUNKS)), dma((2, CHUNKS)), dma((2, half)), dma((2, half)),
                 dma((SWEEPS, ns - 1)), dma((SWEEPS, ns - 1)),
@@ -330,6 +347,27 @@
                                           transcendentals=0),
             name="ridge_sweeps",
         )(x_loc, w_loc.T, y_loc.T, eta_loc.reshape(1, feat_len))
+        pieces = 8
+
+        def put(w_ref, r_ref, w_hbm, r_hbm, sem):
+            width = feat_len // pieces
+            copies = [pltpu.make_async_copy(w_ref.at[:, pl.ds(i * width, width)], w_hbm.at[:, pl.ds(i * width, width)], sem.at[i])
+                      for i in range(pieces)]
+            copies.append(pltpu.make_async_copy(r_ref, r_hbm, sem.at[pieces]))
+            for copy in copies:
+                copy.start()
+            for copy in copies:
+                copy.wait()
+
+        w_out, r_out = pl.pallas_call(
+            put,
+            out_shape=(jax.ShapeDtypeStruct((targets, feat_len), jnp.float32), jax.ShapeDtypeStruct((targets, rows), jnp.float32)),
+            in_specs=[vmem, vmem],
+            out_specs=(hbm, hbm),
+            scratch_shapes=[dma((pieces + 1,))],
+            compiler_params=pltpu.CompilerParams(vmem_limit_bytes=1024 * 1024),
+            name="put_results",
+        )(pltpu.with_memory_space_constraint(w_out, pltpu.VMEM), pltpu.with_memory_space_constraint(r_out, pltpu.VMEM))
         return w_out.T, r_out.T
 
     return jax.shard_map(

time: 591 us -> 586 us (level)
  local copies, waits for them, and re-layouts: 6.77 us -> 0 us
    unnamed x2 -> x0, local copies, waits for them, and re-layouts: 6.77 us -> none
    pallas_call x0 -> x1, Pallas kernels: none -> 5.94 us  [local_solve(): pl.pallas_call(put, out_shape=(jax.ShapeDtypeStruct((targets, feat_len),...]
where the time goes in v3:
time: 586 us; the launch traced here: 585 us
  Pallas kernels  584 us (100%)
    pallas_call x1, Pallas kernels, local_solve(): pl.pallas_call(functools.partial(kernel, ns, nf), out_shape=(pltpu.VMEM((...  579 us

profile of v3, /device:TPU:97, one launch (start us, length us, event | category | flops | bytes accessed | tf_op | source)
XLA Modules:
  0.0 585.1 jit_solution(1088440271514418217)
XLA Ops:
  0.6 578.5 %ridge_sweeps.1 = (f32[32,131072]{1,0:T(8,128)S(1)}, f32[32,128]{1,0:T(8,128)S(1)}) custom-call(bf16[128,131072]{1,0:T(8,128)(2,1)} %x_hbm.1, f32[32,131072]{1,0:T(8,128)} %bitcast.5, f32[32,128]{1,0:T(8,128)} %bitcast.7, f32[1,131072]{1,0:T(1,128)} %bitcast.6), custom_call_target="tpu_custom_call" | custom-call | flops 9663676416 | bytes 100663296 | tf_op jit(solution)/shard_map/ridge_sweeps/pallas_call | solution.py:319
  579.1 5.9 %put_results.1 = (f32[32,131072]{1,0:T(8,128)}, f32[32,128]{1,0:T(8,128)}) custom-call(f32[32,131072]{1,0:T(8,128)S(1)} %get-tuple-element.6.w_ref, f32[32,128]{1,0:T(8,128)S(1)} %get-tuple-element.7.r_ref), custom_call_target="tpu_custom_call" | custom-call | tf_op jit(solution)/shard_map/put_results/pallas_call | solution.py:362

commit v4 on v3

--- a/solution.py
+++ b/solution.py
@@ -18,11 +18,14 @@
 NT = (((1,), (1,)), ((), ()))
 
 
+BLOCK = (0, 2, 1, 3)
+
+
 def far_first(count):
     return sorted(range(1, count), key=lambda o: -min(o, count - o))
 
 
-def kernel(ns, nf, x_hbm, wt_hbm, yt_ref, eta_hbm, wout, rout, xbuf, relay, dbuf, ebuf, vx, vw, usend, rsbuf, agbuf, rbuf, rstate, ucol, urow,
+def kernel(ns, nf, x_hbm, wt_hbm, yt_ref, eta_hbm, wout, rout, relay, xbuf, gbuf, dbuf, ebuf, vx, vw, usend, rsbuf, agbuf, rbuf, rstate, ucol, urow,
            own_sem, w_sem, e_sem, v_sem, rel_s, rel_r, dir_s, dir_r, fwd_s, fwd_r, a_s, a_r, b_s, b_r, c_s, c_r,
            wd_s, wd_r, wf_s, wf_r):
     y, f = lax.axis_index("samp"), lax.axis_index("feat")
@@ -42,7 +45,7 @@
         return pl.ds(pl.multiple_of(owner * own + k * chunk, chunk), chunk)
 
     def rows_of(o):
-        return pl.ds(o * rows, rows)
+        return pl.ds(BLOCK[o] * rows, rows)
 
     def remote(src, dst, send, recv, axis, dev):
         return pltpu.make_async_remote_copy(src_ref=src, dst_ref=dst, send_sem=send, recv_sem=recv,
@@ -131,13 +134,12 @@
         return remote(agbuf.at[t, f], agbuf.at[t, place], b_s.at[t, o - 1], b_r.at[t, o - 1], "feat", lax.rem(f + o, nf))
 
     def c_copy(t, o):
-        return remote(rbuf.at[t, 0], rbuf.at[t, ns - o], c_s.at[t, o - 1], c_r.at[t, o - 1], "samp", lax.rem(y + o, ns))
-
-    def start_a(t):
-        for o in range(1, ns):
-            usend[t, o] = ucol[(o - 1) * rows:o * rows, :].T + urow[:, (o - 1) * rows:o * rows]
-        for o in far_first(ns):
-            a_copy(t, o).start()
+        return remote(rbuf.at[t, 0], rbuf.at[t, BLOCK[ns - o]], c_s.at[t, o - 1], c_r.at[t, o - 1], "samp", lax.rem(y + o, ns))
+
+    def start_a(t, o):
+        place = pl.ds((BLOCK[o] - 1) * rows, rows)
+        usend[t, o] = ucol[place, :].T + urow[:, place]
+        a_copy(t, o).start()
 
     def finish_a(t, total):
         for o in range(1, ns):
@@ -165,7 +167,6 @@
     def finish_c(t):
         for o in range(1, ns):
             c_copy(t, o).wait_recv()
-        return jnp.concatenate([rbuf[t, o] for o in range(ns)], axis=1)
 
     rstate[...] = yt_ref[...] - sum_blocks(0, first)
     start_c(0)
@@ -185,9 +186,17 @@
 
     parts = chunk // sub
 
+    def own_grad(k):
+        for s in range(parts):
+            part = pl.ds(s * sub, sub)
+            gbuf[k, :, part] = jnp.dot(mine_low, xbuf[k, :rows, part], preferred_element_type=jnp.float32)
+
     def advance(k, s, resid):
         part = pl.ds(s * sub, sub)
-        grad = jnp.dot(resid, xbuf[k, :, part], preferred_element_type=jnp.float32) * inv
+        if resid.shape[1] == samples:
+            grad = jnp.dot(resid, xbuf[k, :, part], preferred_element_type=jnp.float32) * inv
+        else:
+            grad = (gbuf[k, :, part] + jnp.dot(resid, xbuf[k, rows:, part], preferred_element_type=jnp.float32)) * inv
         place = pl.ds(pl.multiple_of(y * own + k * chunk + s * sub, sub), sub)
         w_part = wout[:, place]
         delta = ebuf[k, :, part] * (grad - ridge * w_part)
@@ -196,11 +205,11 @@
         dbuf[k, :, part] = low
         return low
 
-    def other_rows(k, low_of):
+    def other_rows(first_row, k, low_of):
         col, row = None, None
         for s in range(parts):
             low = low_of(s)
-            x_part = xbuf[k, rows:, pl.ds(s * sub, sub)]
+            x_part = xbuf[k, first_row:, pl.ds(s * sub, sub)]
             if s < STREAM * parts:
                 term = lax.dot_general(x_part, low, NT, preferred_element_type=jnp.float32)
                 col = term if col is None else col + term
@@ -208,15 +217,38 @@
                 term = lax.dot_general(low, x_part, NT, preferred_element_type=jnp.float32)
                 row = term if row is None else row + term
         if col is not None:
-            ucol[...] += col
+            ucol[first_row - rows:, :] += col
         if row is not None:
-            urow[...] += row
+            urow[:, first_row - rows:] += row
 
     def sweep_chunk(k, resid):
-        other_rows(k, lambda s: advance(k, s, resid))
-
-    def own_rows(k, acc):
-        return acc + lax.dot_general(xbuf[k, :rows, :], dbuf[k], NT, preferred_element_type=jnp.float32)
+        other_rows(rows, k, lambda s: advance(k, s, resid))
+
+    def own_rows(i, acc):
+        for k in (2 * i, 2 * i + 1):
+            for s in range(0, parts, 1):
+                part = pl.ds(s * sub, 1 * sub)
+                acc = acc + lax.dot_general(xbuf[k, :rows, part], dbuf[k, :, part], NT, preferred_element_type=jnp.float32)
+        return acc
+
+    def near_rows(i, carry):
+        col, row = carry
+        for k in (2 * i, 2 * i + 1):
+            col = col + lax.dot_general(xbuf[k, 2 * rows:3 * rows, :], dbuf[k], NT, preferred_element_type=jnp.float32)
+            row = row + lax.dot_general(dbuf[k], xbuf[k, 3 * rows:, :], NT, preferred_element_type=jnp.float32)
+        return col, row
+
+    def pair_rows(first_row, last_row, i):
+        col, row = None, None
+        held, out = pl.ds(first_row, last_row - first_row), pl.ds(first_row - rows, last_row - first_row)
+        for s in range(0, parts, 1):
+            part = pl.ds(s * sub, 1 * sub)
+            term = lax.dot_general(xbuf[2 * i, held, part], dbuf[2 * i, :, part], NT, preferred_element_type=jnp.float32)
+            col = term if col is None else col + term
+            term = lax.dot_general(dbuf[2 * i + 1, :, part], xbuf[2 * i + 1, held, part], NT, preferred_element_type=jnp.float32)
+            row = term if row is None else row + term
+        ucol[out, :] += col
+        urow[:, out] += row
 
     def arriving(i):
         for d in range(2):
@@ -229,12 +261,10 @@
             forward_copy(d, i).wait_recv()
             sweep_chunk(k, resid)
 
-    def from_store(k):
-        other_rows(k, lambda s: dbuf[k, :, pl.ds(s * sub, sub)])
-
-    def staying(k):
-        for s in range(parts):
-            advance(k, s, resid)
+    def staying(i):
+        for k in (2 * i, 2 * i + 1):
+            for s in range(parts):
+                advance(k, s, resid)
 
     def send_w(k):
         for d in range(2):
@@ -249,20 +279,29 @@
             send_w(k - 1)
 
     for t in range(SWEEPS):
-        resid = finish_c(t)
         ucol[...] = jnp.zeros_like(ucol)
         urow[...] = jnp.zeros_like(urow)
+        if t:
+            mine_low = rbuf[t, 0]
+            each(CHUNKS, own_grad)
+        finish_c(t)
+        resid = jnp.concatenate([rbuf[t, b] for b in range(1 if t else 0, ns)], axis=1)
         if t == 0:
             each(half, arriving)
-        elif t < SWEEPS - 1:
-            each(CHUNKS, staying)
-            each(CHUNKS, from_store)
+            start_a(t, 2)
         else:
-            each(CHUNKS, leaving)
-            send_w(CHUNKS - 1)
-            each(CHUNKS, from_store)
-        start_a(t)
-        mine = lax.fori_loop(0, CHUNKS, own_rows, jnp.zeros((rows, targets), jnp.float32)).T
+            if t < SWEEPS - 1:
+                each(half, staying)
+            else:
+                each(CHUNKS, leaving)
+                send_w(CHUNKS - 1)
+            each(half, functools.partial(pair_rows, rows, 2 * rows))
+            start_a(t, 2)
+            zeros = jnp.zeros((rows, targets), jnp.float32), jnp.zeros((targets, rows), jnp.float32)
+            ucol[rows:2 * rows, :], urow[:, 2 * rows:] = lax.fori_loop(0, half, near_rows, zeros)
+        start_a(t, 1)
+        start_a(t, ns - 1)
+        mine = lax.fori_loop(0, half, own_rows, jnp.zeros((rows, targets), jnp.float32)).T
         if t < SWEEPS - 1:
             rstate[...] = rstate[...] - COMBINE_WEIGHT * sum_blocks(t + 1, finish_a(t, mine))
             start_c(t + 1)
@@ -316,14 +355,15 @@
         hbm = pl.BlockSpec(memory_space=pl.ANY)
         vmem = pl.BlockSpec(memory_space=pltpu.VMEM)
         small = feat_len * targets
-        w_out, r_out = pl.pallas_call(
+        w_out, r_out, _ = pl.pallas_call(
             functools.partial(kernel, ns, nf),
-            out_shape=(pltpu.VMEM((targets, feat_len), jnp.float32), pltpu.VMEM((targets, rows), jnp.float32)),
+            out_shape=(pltpu.VMEM((targets, feat_len), jnp.float32), pltpu.VMEM((targets, rows), jnp.float32),
+                       jax.ShapeDtypeStruct((2, half, rows, chunk), jnp.bfloat16)),
             in_specs=[hbm, hbm, vmem, hbm],
-            out_specs=(vmem, vmem),
+            out_specs=(vmem, vmem, hbm),
             scratch_shapes=[
                 pltpu.VMEM((CHUNKS, samples, chunk), jnp.bfloat16),
-                pltpu.VMEM((2, half, rows, chunk), jnp.bfloat16),
+                pltpu.VMEM((CHUNKS, targets, chunk), jnp.float32),
                 pltpu.VMEM((CHUNKS, targets, chunk), jnp.bfloat16),
                 pltpu.VMEM((CHUNKS, 1, chunk), jnp.float32),
                 pltpu.VMEM((V_SLOTS, rows, chunk), jnp.bfloat16),

time: 586 us -> 580 us (0.990)
  no operation moved by 1% of the time
where the time goes in v4:
time: 580 us; the launch traced here: 579 us
  Pallas kernels  579 us (100%)
    pallas_call x1, Pallas kernels, local_solve(): pl.pallas_call(functools.partial(kernel, ns, nf), out_shape=(pltpu.VMEM((...  573 us

profile of v4, /device:TPU:97, one launch (start us, length us, event | category | flops | bytes accessed | tf_op | source)
XLA Modules:
  0.0 579.3 jit_solution(10493860966360401585)
XLA Ops:
  0.6 572.7 %ridge_sweeps.1 = (f32[32,131072]{1,0:T(8,128)S(1)}, f32[32,128]{1,0:T(8,128)S(1)}, bf16[2,8,128,2048]{3,2,1,0:T(8,128)(2,1)}) custom-call(bf16[128,131072]{1,0:T(8,128)(2,1)} %x_hbm.1, f32[32,131072]{1,0:T(8,128)} %bitcast.5, f32[32,128]{1,0:T(8,128)} %bitcast.7, f32[1,131072]{1,0:T(1,128)} %bitcast.6), custom_call_target="tpu_custom_call" | custom-call | flops 9663676416 | bytes 100663296 | tf_op jit(solution)/shard_map/ridge_sweeps/pallas_call | solution.py:358
  573.4 5.9 %put_results.1 = (f32[32,131072]{1,0:T(8,128)}, f32[32,128]{1,0:T(8,128)}) custom-call(f32[32,131072]{1,0:T(8,128)S(1)} %get-tuple-element.6.w_ref, f32[32,128]{1,0:T(8,128)S(1)} %get-tuple-element.7.r_ref), custom_call_target="tpu_custom_call" | custom-call | tf_op jit(solution)/shard_map/put_results/pallas_call | solution.py:402

commit v5 on v4

--- a/solution.py
+++ b/solution.py
@@ -13,6 +13,7 @@
 CHUNKS = 16
 SUB = 512
 STREAM = 0.5
+EARLY = 4
 V_SLOTS = 3
 MESH = pl.DeviceIdType.MESH
 NT = (((1,), (1,)), ((), ()))
@@ -85,23 +86,22 @@
         part = wout.at[:, cols(owner, 2 * i + d)]
         return remote(part, part, wf_s.at[d, i], wf_r.at[d, i], "samp", ring[d])
 
-    def each(count, body):
-        lax.fori_loop(0, count, lambda i, c: (body(i), c)[1], 0)
+    def each(count, body, start=0):
+        lax.fori_loop(start, count, lambda i, c: (body(i), c)[1], 0)
 
     def start_local(k):
         own_copy(k).start()
         w_load(k).start()
         e_load(k).start()
-
-    for k in range(V_SLOTS):
-        for copy in v_load(k, k):
-            copy.start()
 
     barrier = pltpu.get_barrier_semaphore()
     for o in range(1, ns):
         pl.semaphore_signal(barrier, inc=1, device_id={"samp": lax.rem(y + o, ns)}, device_id_type=MESH)
     for o in range(1, nf):
         pl.semaphore_signal(barrier, inc=1, device_id={"feat": lax.rem(f + o, nf)}, device_id_type=MESH)
+    for k in range(V_SLOTS):
+        for copy in v_load(k, k):
+            copy.start()
     pl.semaphore_wait(barrier, ns - 1 + nf - 1)
 
     def start_relay(i):
@@ -164,9 +164,10 @@
         for o in far_first(ns):
             c_copy(t, o).start()
 
-    def finish_c(t):
-        for o in range(1, ns):
+    def finish_c(t, offsets):
+        for o in offsets:
             c_copy(t, o).wait_recv()
+        return jnp.concatenate([rbuf[t, b] for b in sorted(BLOCK[o] for o in offsets)], axis=1)
 
     rstate[...] = yt_ref[...] - sum_blocks(0, first)
     start_c(0)
@@ -186,17 +187,31 @@
 
     parts = chunk // sub
 
-    def own_grad(k):
+    def rows_grad(low, first_row, k, part):
+        held = pl.ds(first_row, low.shape[1])
+        return jnp.dot(low, xbuf[k, held, part], preferred_element_type=jnp.float32)
+
+    def own_grad(low, k):
         for s in range(parts):
             part = pl.ds(s * sub, sub)
-            gbuf[k, :, part] = jnp.dot(mine_low, xbuf[k, :rows, part], preferred_element_type=jnp.float32)
-
-    def advance(k, s, resid):
+            gbuf[k, :, part] = rows_grad(low, 0, k, part)
+
+    def near_grad(low, k):
+        for s in range(parts):
+            part = pl.ds(s * sub, sub)
+            gbuf[k, :, part] += rows_grad(low, 2 * rows, k, part)
+
+    def ready_grad(own_low, near_low, k):
+        own_copy(k).wait()
+        for e in range(2):
+            direct_copy(e, k).wait_recv()
+        for s in range(parts):
+            part = pl.ds(s * sub, sub)
+            gbuf[k, :, part] = rows_grad(own_low, 0, k, part) + rows_grad(near_low, 2 * rows, k, part)
+
+    def advance(k, s, low):
         part = pl.ds(s * sub, sub)
-        if resid.shape[1] == samples:
-            grad = jnp.dot(resid, xbuf[k, :, part], preferred_element_type=jnp.float32) * inv
-        else:
-            grad = (gbuf[k, :, part] + jnp.dot(resid, xbuf[k, rows:, part], preferred_element_type=jnp.float32)) * inv
+        grad = (gbuf[k, :, part] + rows_grad(low, rows, k, part)) * inv
         place = pl.ds(pl.multiple_of(y * own + k * chunk + s * sub, sub), sub)
         w_part = wout[:, place]
         delta = ebuf[k, :, part] * (grad - ridge * w_part)
@@ -221,8 +236,6 @@
         if row is not None:
             urow[:, first_row - rows:] += row
 
-    def sweep_chunk(k, resid):
-        other_rows(rows, k, lambda s: advance(k, s, resid))
 
     def own_rows(i, acc):
         for k in (2 * i, 2 * i + 1):
@@ -250,29 +263,26 @@
         ucol[out, :] += col
         urow[:, out] += row
 
-    def arriving(i):
+    def arriving(low, i):
         for d in range(2):
             k = 2 * i + d
-            own_copy(k).wait()
             w_load(k).wait()
             e_load(k).wait()
-            for e in range(2):
-                direct_copy(e, k).wait_recv()
             forward_copy(d, i).wait_recv()
-            sweep_chunk(k, resid)
-
-    def staying(i):
+            other_rows(rows, k, lambda s: advance(k, s, low))
+
+    def staying(low, i):
         for k in (2 * i, 2 * i + 1):
             for s in range(parts):
-                advance(k, s, resid)
+                advance(k, s, low)
 
     def send_w(k):
         for d in range(2):
             wd_copy(d, k, y).start()
 
-    def leaving(k):
+    def leaving(low, k):
         for s in range(parts):
-            advance(k, s, resid)
+            advance(k, s, low)
 
         @pl.when(k > 0)
         def _():
@@ -281,19 +291,23 @@
     for t in range(SWEEPS):
         ucol[...] = jnp.zeros_like(ucol)
         urow[...] = jnp.zeros_like(urow)
-        if t:
-            mine_low = rbuf[t, 0]
-            each(CHUNKS, own_grad)
-        finish_c(t)
-        resid = jnp.concatenate([rbuf[t, b] for b in range(1 if t else 0, ns)], axis=1)
         if t == 0:
-            each(half, arriving)
+            near = finish_c(t, (1, ns - 1))
+            each(CHUNKS, functools.partial(ready_grad, rbuf[t, 0], near))
+            each(half, functools.partial(arriving, finish_c(t, (2,))))
             start_a(t, 2)
         else:
+            each(CHUNKS, functools.partial(own_grad, rbuf[t, 0]))
+            near = finish_c(t, (1, ns - 1))
+            each(EARLY, functools.partial(near_grad, near))
+            far_low = finish_c(t, (2,))
+            other_low = jnp.concatenate([far_low, near], axis=1)
             if t < SWEEPS - 1:
-                each(half, staying)
+                each(EARLY // 2, functools.partial(staying, far_low))
+                each(half, functools.partial(staying, other_low), EARLY // 2)
             else:
-                each(CHUNKS, leaving)
+                each(EARLY, functools.partial(leaving, far_low))
+                each(CHUNKS, functools.partial(leaving, other_low), EARLY)
                 send_w(CHUNKS - 1)
             each(half, functools.partial(pair_rows, rows, 2 * rows))
             start_a(t, 2)
@@ -319,17 +333,20 @@
     each(half, start_wf_pair)
     rout[...] = rstate[...] - COMBINE_WEIGHT * sum_blocks(SWEEPS, finish_a(SWEEPS - 1, mine))
 
+    def finish_full(k):
+        for d in range(2):
+            direct_copy(d, k).wait_send()
+            wd_copy(d, k, y).wait_send()
+
     def finish_half(i):
         for d in range(2):
             relay_copy(d, i).wait_send()
             forward_copy(d, i).wait_send()
+
+    def finish_last(i):
+        for d in range(2):
+            wf_copy(d, i, ring[1 - d]).wait_send()
             wf_copy(d, i, far).wait_recv()
-            wf_copy(d, i, ring[1 - d]).wait_send()
-
-    def finish_full(k):
-        for d in range(2):
-            direct_copy(d, k).wait_send()
-            wd_copy(d, k, y).wait_send()
 
     each(CHUNKS, finish_full)
     each(half, finish_half)
@@ -340,6 +357,7 @@
     for t in range(SWEEPS + 1):
         for o in range(1, nf):
             b_copy(t, o, f).wait_send()
+    each(half, finish_last)
 
 
 def solution(mesh):
@@ -387,11 +405,11 @@
                                           transcendentals=0),
             name="ridge_sweeps",
         )(x_loc, w_loc.T, y_loc.T, eta_loc.reshape(1, feat_len))
-        pieces = 8
+        pieces = targets // 8
 
         def put(w_ref, r_ref, w_hbm, r_hbm, sem):
-            width = feat_len // pieces
-            copies = [pltpu.make_async_copy(w_ref.at[:, pl.ds(i * width, width)], w_hbm.at[:, pl.ds(i * width, width)], sem.at[i])
+            width = targets // pieces
+            copies = [pltpu.make_async_copy(w_ref.at[pl.ds(i * width, width), :], w_hbm.at[pl.ds(i * width, width), :], sem.at[i])
                       for i in range(pieces)]
             copies.append(pltpu.make_async_copy(r_ref, r_hbm, sem.at[pieces]))
             for copy in copies:

time: 580 us -> 581 us (level)
  no operation moved by 1% of the time
where the time goes in v5:
time: 581 us
  Pallas kernels  580 us (100%)
    pallas_call x1, Pallas kernels, local_solve(): pl.pallas_call(functools.partial(kernel, ns, nf), out_shape=(pltpu.VMEM((...  574 us

profile of v5, /device:TPU:97, one launch (start us, length us, event | category | flops | bytes accessed | tf_op | source)
XLA Modules:
  0.0 580.6 jit_solution(13686485154154138865)
XLA Ops:
  0.6 574.0 %ridge_sweeps.1 = (f32[32,131072]{1,0:T(8,128)S(1)}, f32[32,128]{1,0:T(8,128)S(1)}, bf16[2,8,128,2048]{3,2,1,0:T(8,128)(2,1)}) custom-call(bf16[128,131072]{1,0:T(8,128)(2,1)} %x_hbm.1, f32[32,131072]{1,0:T(8,128)} %bitcast.5, f32[32,128]{1,0:T(8,128)} %bitcast.7, f32[1,131072]{1,0:T(1,128)} %bitcast.6), custom_call_target="tpu_custom_call" | custom-call | flops 9663676416 | bytes 100663296 | tf_op jit(solution)/shard_map/ridge_sweeps/pallas_call | solution.py:376
  574.6 6.0 %put_results.1 = (f32[32,131072]{1,0:T(8,128)}, f32[32,128]{1,0:T(8,128)}) custom-call(f32[32,131072]{1,0:T(8,128)S(1)} %get-tuple-element.6.w_ref, f32[32,128]{1,0:T(8,128)S(1)} %get-tuple-element.7.r_ref), custom_call_target="tpu_custom_call" | custom-call | tf_op jit(solution)/shard_map/put_results/pallas_call | solution.py:420

commit v6 on v5

--- a/solution.py
+++ b/solution.py
@@ -13,7 +13,6 @@
 CHUNKS = 16
 SUB = 512
 STREAM = 0.5
-EARLY = 4
 V_SLOTS = 3
 MESH = pl.DeviceIdType.MESH
 NT = (((1,), (1,)), ((), ()))
@@ -86,8 +85,8 @@
         part = wout.at[:, cols(owner, 2 * i + d)]
         return remote(part, part, wf_s.at[d, i], wf_r.at[d, i], "samp", ring[d])
 
-    def each(count, body, start=0):
-        lax.fori_loop(start, count, lambda i, c: (body(i), c)[1], 0)
+    def each(count, body):
+        lax.fori_loop(0, count, lambda i, c: (body(i), c)[1], 0)
 
     def start_local(k):
         own_copy(k).start()
@@ -195,11 +194,6 @@
         for s in range(parts):
             part = pl.ds(s * sub, sub)
             gbuf[k, :, part] = rows_grad(low, 0, k, part)
-
-    def near_grad(low, k):
-        for s in range(parts):
-            part = pl.ds(s * sub, sub)
-            gbuf[k, :, part] += rows_grad(low, 2 * rows, k, part)
 
     def ready_grad(own_low, near_low, k):
         own_copy(k).wait()
@@ -298,16 +292,11 @@
             start_a(t, 2)
         else:
             each(CHUNKS, functools.partial(own_grad, rbuf[t, 0]))
-            near = finish_c(t, (1, ns - 1))
-            each(EARLY, functools.partial(near_grad, near))
-            far_low = finish_c(t, (2,))
-            other_low = jnp.concatenate([far_low, near], axis=1)
+            other_low = finish_c(t, (1, 2, ns - 1))
             if t < SWEEPS - 1:
-                each(EARLY // 2, functools.partial(staying, far_low))
-                each(half, functools.partial(staying, other_low), EARLY // 2)
+                each(half, functools.partial(staying, other_low))
             else:
-                each(EARLY, functools.partial(leaving, far_low))
-                each(CHUNKS, functools.partial(leaving, other_low), EARLY)
+                each(CHUNKS, functools.partial(leaving, other_low))
                 send_w(CHUNKS - 1)
             each(half, functools.partial(pair_rows, rows, 2 * rows))
             start_a(t, 2)
@@ -405,11 +394,11 @@
                                           transcendentals=0),
             name="ridge_sweeps",
         )(x_loc, w_loc.T, y_loc.T, eta_loc.reshape(1, feat_len))
-        pieces = targets // 8
+        pieces = 8
 
         def put(w_ref, r_ref, w_hbm, r_hbm, sem):
-            width = targets // pieces
-            copies = [pltpu.make_async_copy(w_ref.at[pl.ds(i * width, width), :], w_hbm.at[pl.ds(i * width, width), :], sem.at[i])
+            width = feat_len // pieces
+            copies = [pltpu.make_async_copy(w_ref.at[:, pl.ds(i * width, width)], w_hbm.at[:, pl.ds(i * width, width)], sem.at[i])
                       for i in range(pieces)]
             copies.append(pltpu.make_async_copy(r_ref, r_hbm, sem.at[pieces]))
             for copy in copies:

time: 581 us -> 580 us (level)
  no operation moved by 1% of the time
where the time goes in v6:
time: 580 us; the launch traced here: 579 us
  Pallas kernels  578 us (100%)
    pallas_call x1, Pallas kernels, local_solve(): pl.pallas_call(functools.partial(kernel, ns, nf), out_shape=(pltpu.VMEM((...  572 us

profile of v6, /device:TPU:97, one launch (start us, length us, event | category | flops | bytes accessed | tf_op | source)
XLA Modules:
  0.0 578.8 jit_solution(14596760773530454208)
XLA Ops:
  0.6 572.3 %ridge_sweeps.1 = (f32[32,131072]{1,0:T(8,128)S(1)}, f32[32,128]{1,0:T(8,128)S(1)}, bf16[2,8,128,2048]{3,2,1,0:T(8,128)(2,1)}) custom-call(bf16[128,131072]{1,0:T(8,128)(2,1)} %x_hbm.1, f32[32,131072]{1,0:T(8,128)} %bitcast.5, f32[32,128]{1,0:T(8,128)} %bitcast.7, f32[1,131072]{1,0:T(1,128)} %bitcast.6), custom_call_target="tpu_custom_call" | custom-call | flops 9663676416 | bytes 100663296 | tf_op jit(solution)/shard_map/ridge_sweeps/pallas_call | solution.py:365
  572.9 5.9 %put_results.1 = (f32[32,131072]{1,0:T(8,128)}, f32[32,128]{1,0:T(8,128)}) custom-call(f32[32,131072]{1,0:T(8,128)S(1)} %get-tuple-element.6.w_ref, f32[32,128]{1,0:T(8,128)S(1)} %get-tuple-element.7.r_ref), custom_call_target="tpu_custom_call" | custom-call | tf_op jit(solution)/shard_map/put_results/pallas_call | solution.py:409

commit v7 on v6

--- a/solution.py
+++ b/solution.py
@@ -33,7 +33,7 @@
     targets = wt_hbm.shape[0]
     own = feat_len // ns
     chunk = own // CHUNKS
-    half = CHUNKS // 2
+    half, quarter = CHUNKS // 2, CHUNKS // 4
     sub = min(SUB, chunk)
     samples = rows * ns
     inv = 1.0 / samples
@@ -44,6 +44,12 @@
     def cols(owner, k):
         return pl.ds(pl.multiple_of(owner * own + k * chunk, chunk), chunk)
 
+    def block_cols(owner, i):
+        return pl.ds(pl.multiple_of(owner * own + i * 2 * chunk, 2 * chunk), 2 * chunk)
+
+    def lanes(h, part):
+        return pl.ds(h * chunk + part.start, part.size)
+
     def rows_of(o):
         return pl.ds(BLOCK[o] * rows, rows)
 
@@ -51,8 +57,8 @@
         return pltpu.make_async_remote_copy(src_ref=src, dst_ref=dst, send_sem=send, recv_sem=recv,
                                             device_id={axis: dev}, device_id_type=MESH)
 
-    def own_copy(k):
-        return pltpu.make_async_copy(x_hbm.at[:, cols(y, k)], xbuf.at[k, rows_of(0), :], own_sem.at[k])
+    def own_copy(i):
+        return pltpu.make_async_copy(x_hbm.at[:, block_cols(y, i)], xbuf.at[i, rows_of(0), :], own_sem.at[i])
 
     def w_load(k):
         return pltpu.make_async_copy(wt_hbm.at[:, cols(y, k)], wout.at[:, cols(y, k)], w_sem.at[k])
@@ -69,14 +75,16 @@
         return (pltpu.make_async_copy(x_hbm.at[:, v_cols(k)], vx.at[slot], v_sem.at[0, slot]),
                 pltpu.make_async_copy(wt_hbm.at[:, v_cols(k)], vw.at[slot], v_sem.at[1, slot]))
 
-    def relay_copy(d, i):
-        return remote(x_hbm.at[:, cols(far, 2 * i + d)], relay.at[d, i], rel_s.at[d, i], rel_r.at[d, i], "samp", ring[d])
-
-    def direct_copy(d, k):
-        return remote(x_hbm.at[:, cols(ring[d], k)], xbuf.at[k, rows_of((ns - 1, 1)[d]), :], dir_s.at[d, k], dir_r.at[d, k], "samp", ring[d])
-
-    def forward_copy(d, i):
-        return remote(relay.at[d, i], xbuf.at[2 * i + d, rows_of(2), :], fwd_s.at[d, i], fwd_r.at[d, i], "samp", ring[d])
+    def relay_copy(d, p):
+        return remote(x_hbm.at[:, block_cols(far, 2 * p + d)], relay.at[d, p], rel_s.at[d, p], rel_r.at[d, p], "samp", ring[d])
+
+    def direct_copy(d, i):
+        return remote(x_hbm.at[:, block_cols(ring[d], i)], xbuf.at[i, rows_of((ns - 1, 1)[d]), :], dir_s.at[d, i], dir_r.at[d, i],
+                      "samp", ring[d])
+
+    def forward_copy(d, p, h):
+        return remote(relay.at[d, p, :, pl.ds(h * chunk, chunk)], xbuf.at[2 * p + d, rows_of(2), pl.ds(h * chunk, chunk)],
+                      fwd_s.at[d, 2 * p + h], fwd_r.at[d, 2 * p + h], "samp", ring[d])
 
     def wd_copy(d, k, owner):
         return remote(wout.at[:, cols(y, k)], wout.at[:, cols(owner, k)], wd_s.at[d, k], wd_r.at[d, k], "samp", ring[d])
@@ -89,7 +97,6 @@
         lax.fori_loop(0, count, lambda i, c: (body(i), c)[1], 0)
 
     def start_local(k):
-        own_copy(k).start()
         w_load(k).start()
         e_load(k).start()
 
@@ -107,7 +114,7 @@
         for d in range(2):
             relay_copy(d, i).start()
 
-    each(half, start_relay)
+    each(quarter, start_relay)
 
     def v_step(k, acc):
         slot = lax.rem(k, V_SLOTS)
@@ -124,6 +131,7 @@
         return acc
 
     first = lax.fori_loop(0, v_steps, v_step, jnp.zeros((targets, rows), jnp.float32))
+    each(half, lambda i: own_copy(i).start())
     each(CHUNKS, start_local)
 
     def a_copy(t, o):
@@ -175,37 +183,42 @@
         for d in range(2):
             direct_copy(d, k).start()
 
-    each(CHUNKS, start_direct)
-
-    def start_forward(i):
-        for d in range(2):
-            relay_copy(d, i).wait_recv()
-            forward_copy(d, i).start()
-
-    each(half, start_forward)
+    each(half, start_direct)
+
+    def start_forward(p):
+        for d in range(2):
+            relay_copy(d, p).wait_recv()
+        for h in range(2):
+            for d in range(2):
+                forward_copy(d, p, h).start()
+
+    each(quarter, start_forward)
 
     parts = chunk // sub
 
-    def rows_grad(low, first_row, k, part):
+    def rows_grad(low, first_row, i, h, part):
         held = pl.ds(first_row, low.shape[1])
-        return jnp.dot(low, xbuf[k, held, part], preferred_element_type=jnp.float32)
-
-    def own_grad(low, k):
-        for s in range(parts):
-            part = pl.ds(s * sub, sub)
-            gbuf[k, :, part] = rows_grad(low, 0, k, part)
-
-    def ready_grad(own_low, near_low, k):
-        own_copy(k).wait()
+        return jnp.dot(low, xbuf[i, held, lanes(h, part)], preferred_element_type=jnp.float32)
+
+    def own_grad(low, i):
+        for h in range(2):
+            for s in range(parts):
+                part = pl.ds(s * sub, sub)
+                gbuf[2 * i + h, :, part] = rows_grad(low, 0, i, h, part)
+
+    def ready_grad(own_low, near_low, i):
+        own_copy(i).wait()
         for e in range(2):
-            direct_copy(e, k).wait_recv()
-        for s in range(parts):
-            part = pl.ds(s * sub, sub)
-            gbuf[k, :, part] = rows_grad(own_low, 0, k, part) + rows_grad(near_low, 2 * rows, k, part)
-
-    def advance(k, s, low):
+            direct_copy(e, i).wait_recv()
+        for h in range(2):
+            for s in range(parts):
+                part = pl.ds(s * sub, sub)
+                gbuf[2 * i + h, :, part] = rows_grad(own_low, 0, i, h, part) + rows_grad(near_low, 2 * rows, i, h, part)
+
+    def advance(i, h, s, low):
+        k = 2 * i + h
         part = pl.ds(s * sub, sub)
-        grad = (gbuf[k, :, part] + rows_grad(low, rows, k, part)) * inv
+        grad = (gbuf[k, :, part] + rows_grad(low, rows, i, h, part)) * inv
         place = pl.ds(pl.multiple_of(y * own + k * chunk + s * sub, sub), sub)
         w_part = wout[:, place]
         delta = ebuf[k, :, part] * (grad - ridge * w_part)
@@ -214,11 +227,11 @@
         dbuf[k, :, part] = low
         return low
 
-    def other_rows(first_row, k, low_of):
+    def other_rows(first_row, i, h, low_of):
         col, row = None, None
         for s in range(parts):
             low = low_of(s)
-            x_part = xbuf[k, first_row:, pl.ds(s * sub, sub)]
+            x_part = xbuf[i, first_row:, lanes(h, pl.ds(s * sub, sub))]
             if s < STREAM * parts:
                 term = lax.dot_general(x_part, low, NT, preferred_element_type=jnp.float32)
                 col = term if col is None else col + term
@@ -232,17 +245,18 @@
 
 
     def own_rows(i, acc):
-        for k in (2 * i, 2 * i + 1):
+        for h in range(2):
             for s in range(0, parts, 1):
                 part = pl.ds(s * sub, 1 * sub)
-                acc = acc + lax.dot_general(xbuf[k, :rows, part], dbuf[k, :, part], NT, preferred_element_type=jnp.float32)
+                acc = acc + lax.dot_general(xbuf[i, :rows, lanes(h, part)], dbuf[2 * i + h, :, part], NT, preferred_element_type=jnp.float32)
         return acc
 
     def near_rows(i, carry):
         col, row = carry
-        for k in (2 * i, 2 * i + 1):
-            col = col + lax.dot_general(xbuf[k, 2 * rows:3 * rows, :], dbuf[k], NT, preferred_element_type=jnp.float32)
-            row = row + lax.dot_general(dbuf[k], xbuf[k, 3 * rows:, :], NT, preferred_element_type=jnp.float32)
+        for h in range(2):
+            k, held = 2 * i + h, pl.ds(h * chunk, chunk)
+            col = col + lax.dot_general(xbuf[i, 2 * rows:3 * rows, held], dbuf[k], NT, preferred_element_type=jnp.float32)
+            row = row + lax.dot_general(dbuf[k], xbuf[i, 3 * rows:, held], NT, preferred_element_type=jnp.float32)
         return col, row
 
     def pair_rows(first_row, last_row, i):
@@ -250,53 +264,58 @@
         held, out = pl.ds(first_row, last_row - first_row), pl.ds(first_row - rows, last_row - first_row)
         for s in range(0, parts, 1):
             part = pl.ds(s * sub, 1 * sub)
-            term = lax.dot_general(xbuf[2 * i, held, part], dbuf[2 * i, :, part], NT, preferred_element_type=jnp.float32)
+            term = lax.dot_general(xbuf[i, held, lanes(0, part)], dbuf[2 * i, :, part], NT, preferred_element_type=jnp.float32)
             col = term if col is None else col + term
-            term = lax.dot_general(dbuf[2 * i + 1, :, part], xbuf[2 * i + 1, held, part], NT, preferred_element_type=jnp.float32)
+            term = lax.dot_general(dbuf[2 * i + 1, :, part], xbuf[i, held, lanes(1, part)], NT, preferred_element_type=jnp.float32)
             row = term if row is None else row + term
         ucol[out, :] += col
         urow[:, out] += row
 
-    def arriving(low, i):
-        for d in range(2):
-            k = 2 * i + d
-            w_load(k).wait()
-            e_load(k).wait()
-            forward_copy(d, i).wait_recv()
-            other_rows(rows, k, lambda s: advance(k, s, low))
+    def arriving(low, p):
+        for h in range(2):
+            for d in range(2):
+                i = 2 * p + d
+                w_load(2 * i + h).wait()
+                e_load(2 * i + h).wait()
+                forward_copy(d, p, h).wait_recv()
+                other_rows(rows, i, h, lambda s: advance(i, h, s, low))
 
     def staying(low, i):
-        for k in (2 * i, 2 * i + 1):
+        for h in range(2):
             for s in range(parts):
-                advance(k, s, low)
+                advance(i, h, s, low)
 
     def send_w(k):
         for d in range(2):
             wd_copy(d, k, y).start()
 
-    def leaving(low, k):
+    def leaving(low, i):
         for s in range(parts):
-            advance(k, s, low)
-
-        @pl.when(k > 0)
+            advance(i, 0, s, low)
+
+        @pl.when(i > 0)
         def _():
-            send_w(k - 1)
+            send_w(2 * i - 1)
+
+        for s in range(parts):
+            advance(i, 1, s, low)
+        send_w(2 * i)
 
     for t in range(SWEEPS):
         ucol[...] = jnp.zeros_like(ucol)
         urow[...] = jnp.zeros_like(urow)
         if t == 0:
             near = finish_c(t, (1, ns - 1))
-            each(CHUNKS, functools.partial(ready_grad, rbuf[t, 0], near))
-            each(half, functools.partial(arriving, finish_c(t, (2,))))
+            each(half, functools.partial(ready_grad, rbuf[t, 0], near))
+            each(quarter, functools.partial(arriving, finish_c(t, (2,))))
             start_a(t, 2)
         else:
-            each(CHUNKS, functools.partial(own_grad, rbuf[t, 0]))
+            each(half, functools.partial(own_grad, rbuf[t, 0]))
             other_low = finish_c(t, (1, 2, ns - 1))
             if t < SWEEPS - 1:
                 each(half, functools.partial(staying, other_low))
             else:
-                each(CHUNKS, functools.partial(leaving, other_low))
+                each(half, functools.partial(leaving, other_low))
                 send_w(CHUNKS - 1)
             each(half, functools.partial(pair_rows, rows, 2 * rows))
             start_a(t, 2)
@@ -324,13 +343,17 @@
 
     def finish_full(k):
         for d in range(2):
-            direct_copy(d, k).wait_send()
             wd_copy(d, k, y).wait_send()
 
     def finish_half(i):
         for d in range(2):
-            relay_copy(d, i).wait_send()
-            forward_copy(d, i).wait_send()
+            direct_copy(d, i).wait_send()
+
+    def finish_quarter(p):
+        for d in range(2):
+            relay_copy(d, p).wait_send()
+            for h in range(2):
+                forward_copy(d, p, h).wait_send()
 
     def finish_last(i):
         for d in range(2):
@@ -339,6 +362,7 @@
 
     each(CHUNKS, finish_full)
     each(half, finish_half)
+    each(quarter, finish_quarter)
     for t in range(SWEEPS):
         for o in range(1, ns):
             a_copy(t, o).wait_send()
@@ -357,7 +381,7 @@
         targets = w_loc.shape[1]
         samples = rows * ns
         chunk = feat_len // ns // CHUNKS
-        half = CHUNKS // 2
+        half, quarter = CHUNKS // 2, CHUNKS // 4
         dma = pltpu.SemaphoreType.DMA
         hbm = pl.BlockSpec(memory_space=pl.ANY)
         vmem = pl.BlockSpec(memory_space=pltpu.VMEM)
@@ -365,11 +389,11 @@
         w_out, r_out, _ = pl.pallas_call(
             functools.partial(kernel, ns, nf),
             out_shape=(pltpu.VMEM((targets, feat_len), jnp.float32), pltpu.VMEM((targets, rows), jnp.float32),
-                       jax.ShapeDtypeStruct((2, half, rows, chunk), jnp.bfloat16)),
+                       jax.ShapeDtypeStruct((2, quarter, rows, 2 * chunk), jnp.bfloat16)),
             in_specs=[hbm, hbm, vmem, hbm],
             out_specs=(vmem, vmem, hbm),
             scratch_shapes=[
-                pltpu.VMEM((CHUNKS, samples, chunk), jnp.bfloat16),
+                pltpu.VMEM((half, samples, 2 * chunk), jnp.bfloat16),
                 pltpu.VMEM((CHUNKS, targets, chunk), jnp.float32),
                 pltpu.VMEM((CHUNKS, targets, chunk), jnp.bfloat16),
                 pltpu.VMEM((CHUNKS, 1, chunk), jnp.float32),
@@ -382,8 +406,8 @@
                 pltpu.VMEM((targets, rows), jnp.float32),
                 pltpu.VMEM((samples - rows, targets), jnp.float32),
                 pltpu.VMEM((targets, samples - rows), jnp.float32),
-                dma((CHUNKS,)), dma((CHUNKS,)), dma((CHUNKS,)), dma((2, V_SLOTS)),
-                dma((2, half)), dma((2, half)), dma((2, CHUNKS)), dma((2, CHUNKS)), dma((2, half)), dma((2, half)),
+                dma((half,)), dma((CHUNKS,)), dma((CHUNKS,)), dma((2, V_SLOTS)),
+                dma((2, quarter)), dma((2, quarter)), dma((2, half)), dma((2, half)), dma((2, half)), dma((2, half)),
                 dma((SWEEPS, ns - 1)), dma((SWEEPS, ns - 1)),
                 dma((SWEEPS + 1, nf - 1)), dma((SWEEPS + 1, nf - 1)),
                 dma((SWEEPS, ns - 1)), dma((SWEEPS, ns - 1)),

time: 580 us -> 577 us (level)
  no operation moved by 1% of the time
where the time goes in v7:
time: 577 us
  Pallas kernels  576 us (100%)
    pallas_call x1, Pallas kernels, local_solve(): pl.pallas_call(functools.partial(kernel, ns, nf), out_shape=(pltpu.VMEM((...  570 us

profile of v7, /device:TPU:97, one launch (start us, length us, event | category | flops | bytes accessed | tf_op | source)
XLA Modules:
  0.0 576.5 jit_solution(17827897530225337305)
XLA Ops:
  0.6 570.0 %ridge_sweeps.1 = (f32[32,131072]{1,0:T(8,128)S(1)}, f32[32,128]{1,0:T(8,128)S(1)}, bf16[2,4,128,4096]{3,2,1,0:T(8,128)(2,1)}) custom-call(bf16[128,131072]{1,0:T(8,128)(2,1)} %x_hbm.1, f32[32,131072]{1,0:T(8,128)} %bitcast.5, f32[32,128]{1,0:T(8,128)} %bitcast.7, f32[1,131072]{1,0:T(1,128)} %bitcast.6), custom_call_target="tpu_custom_call" | custom-call | flops 9663676416 | bytes 100663296 | tf_op jit(solution)/shard_map/ridge_sweeps/pallas_call | solution.py:389
  570.6 5.9 %put_results.1 = (f32[32,131072]{1,0:T(8,128)}, f32[32,128]{1,0:T(8,128)}) custom-call(f32[32,131072]{1,0:T(8,128)S(1)} %get-tuple-element.6.w_ref, f32[32,128]{1,0:T(8,128)S(1)} %get-tuple-element.7.r_ref), custom_call_target="tpu_custom_call" | custom-call | tf_op jit(solution)/shard_map/put_results/pallas_call | solution.py:433
